TPU v7x, 128 devices: a whole 4x4x4 slice. The times are simulated.
128 devices in a mesh: space: 32 (over z, y, core), freq: 4 (over x).
Axes of the slice: x: 4, y: 4, z: 4, core: 2. Of those that a mesh axis runs over, the one named last changes fastest.
Arguments:
- coeffs: bfloat16 [128, 2, 64, 49152], P('freq', None, None, 'space'), may hold values from -6 to 6
- weights: float32 [49152], P('space'), may hold values from 0.25 to 4
- mode_counts: int32 [128], replicated, may hold values from 4 to 64
- owner_order: int32 [128], replicated, may hold values from 0 to 127, as said below
Outputs:
- mode_fields: bfloat16 [128, 2, 64, 49152], P('freq', None, None, 'space')
- spectrum: float32 [128, 64], P(('space', 'freq'))
- energy: float32 [64], replicated
Inputs may be any that keep to these rules, and one draw needn't show every extreme that they name: `owner_order`: A permutation of the frequencies in which slot r holds a frequency f with f // 32 == (r) % 4.
All inputs are finite; a program needn't handle non-finite values.
Results may differ from a plain program's by a relative error of at most 0.0047.
Values may be sent and summed in bfloat16 or wider, within the bound.
No kernel may reach another device: no remote copies, remote signals or barrier semaphores. Data moves between devices by JAX's collectives and lax.ppermute only.
A program may use at most 128 MiB of HBM per device.

v0:
```python
import functools

import jax
import jax.numpy as jnp
from jax import lax
from jax.sharding import Mesh
from jax.sharding import PartitionSpec as P

F = 128
M = 64
ITERS = 3
SPACE = ("space_0", "space_1", "space_2")
SPACE_FREQ = ("space_0", "space_1", "space_2", "freq")


def in_blocks(shard, dim, count):
    before, after = (shard.shape[:dim], shard.shape[dim + 1 :])
    return jnp.moveaxis(shard.reshape(*before, count, -1, *after), dim, 0)


def sum_at_owner(shard, axis, dim):
    parts = in_blocks(shard, dim, lax.axis_size(axis))
    arrived = lax.all_to_all(parts, axis, split_axis=0, concat_axis=0, tiled=True)
    return arrived.sum(axis=0)


def shortened(shard):
    return jax.tree.map(lambda a: a.astype(jnp.bfloat16) if a.dtype == jnp.float32 else a, shard)


def laid_out(parts, dim):
    shape = list(parts.shape[1:])
    shape[dim] *= parts.shape[0]
    return jnp.moveaxis(parts, 0, dim).reshape(shape)


def sent_to_all(shard, axis):
    count = lax.axis_size(axis)
    return lax.all_to_all(
        jnp.broadcast_to(shard[None], (count, *shard.shape)), axis, 0, 0, tiled=True
    )


def gathered_copies(shard, axis, dim):
    return laid_out(sent_to_all(shard, axis), dim)


def by_axis(shard, axes):
    return functools.reduce(lax.psum, axes, shard)


def assemble(real_part, imag_part):
    half_n = real_part.shape[0]
    real_part = 0.5 * (real_part + real_part.T)
    imag_part = 0.5 * (imag_part - imag_part.T)
    upper_rows = jnp.concatenate([real_part, -imag_part], axis=1)
    bottom = jnp.concatenate([imag_part, real_part], axis=1)
    return (jnp.concatenate([upper_rows, bottom], axis=0), jnp.trace(real_part) / half_n)


def embed_folded(folded):
    return assemble(folded[0], folded[1])


def fold_products(products):
    half_n = products.shape[1] // 2
    real_part = products[:, :half_n, :half_n] + products[:, half_n:, half_n:]
    imag_part = products[:, :half_n, half_n:] - products[:, half_n:, :half_n]
    return jnp.stack([real_part, imag_part], axis=1)


def iterate(hermit, shift_val):
    basis_cols = jnp.eye(hermit.shape[0], M, dtype=jnp.float32)
    for sweep_index in range(ITERS):
        image_cols = (
            jnp.dot(hermit, basis_cols, precision=lax.Precision.HIGHEST) + shift_val * basis_cols
        )
        gram_mat = jnp.dot(image_cols.T, image_cols, precision=lax.Precision.HIGHEST)
        lower_tri = jnp.linalg.cholesky(gram_mat)
        basis_cols = lax.linalg.triangular_solve(
            lower_tri, image_cols, left_side=False, lower=True, transpose_a=True
        )
    ritz_vals = jnp.sum(
        basis_cols * jnp.dot(hermit, basis_cols, precision=lax.Precision.HIGHEST), axis=0
    )
    return (basis_cols, ritz_vals)


def expand(basis_cols, kept_cols):
    half_n = basis_cols.shape[0] // 2
    real_cols = basis_cols[:half_n] * kept_cols
    imag_cols = basis_cols[half_n:] * kept_cols
    expander = jnp.concatenate(
        [
            jnp.concatenate([real_cols, imag_cols], axis=1),
            jnp.concatenate([-imag_cols, real_cols], axis=1),
        ],
        axis=0,
    )
    return expander.T.astype(jnp.bfloat16)


def weighted_grams(coeff_rows, cell_weights):
    weighted = (coeff_rows * cell_weights).astype(jnp.bfloat16)
    count_rows = coeff_rows.shape[0]
    flat_rows = coeff_rows.reshape(count_rows, 2 * coeff_rows.shape[2], coeff_rows.shape[3])
    flat_weighted = weighted.reshape(flat_rows.shape)
    return jnp.einsum("nax,nbx->nab", flat_rows, flat_weighted, preferred_element_type=jnp.float32)


def solve_slots(hermit, shift_val, kept_cols):
    basis_cols, ritz_vals = jax.vmap(iterate)(hermit, shift_val)
    expander = jax.vmap(expand)(basis_cols, kept_cols)
    return (expander, ritz_vals * kept_cols)


def shards(coeffs, weights, mode_counts, owner_order):
    space_count = lax.axis_size(SPACE)
    freq_count = lax.axis_size("freq")
    group_index = lax.axis_index("freq")
    space_index = lax.axis_index(SPACE)
    fgroup, _, blocks, points = coeffs.shape
    per_dev = fgroup // space_count
    total_x = points * space_count
    positions = jnp.arange(fgroup, dtype=jnp.int32)
    slot_send = (positions // per_dev * freq_count + group_index) * per_dev + positions % per_dev
    rows_send = owner_order[slot_send] - group_index * fgroup
    inverse = jnp.argsort(rows_send)
    slot_own = (space_index * freq_count + group_index) * per_dev + jnp.arange(
        per_dev, dtype=jnp.int32
    )
    count_own = mode_counts[owner_order[slot_own]]
    kept_cols = (jnp.arange(M, dtype=jnp.int32)[None, :] < count_own[:, None]).astype(jnp.float32)
    cell_weights = weights / total_x
    grams = weighted_grams(jnp.take(coeffs, rows_send, axis=0), cell_weights)
    summed = sum_at_owner(fold_products(grams), SPACE, 0)
    hermit, shift_val = jax.vmap(embed_folded)(summed)
    expander, ritz_vals = solve_slots(hermit, shift_val, kept_cols)
    all_bases = jax.tree.map(
        lambda part, own: part.astype(own.dtype),
        jax.tree.map(lambda part: gathered_copies(part, SPACE, 0), shortened(expander)),
        expander,
    )
    own_bases = jnp.take(all_bases, inverse, axis=0)
    flat_rows = coeffs.reshape(fgroup, 2 * blocks, points)
    mode_fields = jnp.einsum(
        "nmb,nbx->nmx", own_bases, flat_rows, preferred_element_type=jnp.float32
    ).astype(jnp.bfloat16)
    mode_fields = mode_fields.reshape(fgroup, 2, M, points)
    energy = by_axis(jnp.sum(ritz_vals, axis=0), SPACE_FREQ) / F
    return (mode_fields, ritz_vals, energy)


def solution(mesh):
    split = Mesh(
        mesh.devices.reshape(4, 4, 2, mesh.shape["freq"]), ("space_0", "space_1", "space_2", "freq")
    )
    placed = (P("freq", None, None, SPACE), P(SPACE), P(), P())
    return jax.shard_map(
        shards,
        mesh=split,
        in_specs=placed,
        out_specs=(P("freq", None, None, SPACE), P(SPACE_FREQ, None), P()),
        check_vma=False,
    )
```

profile of v0, /device:TPU:0, one launch (start us, length us, event | category | flops | bytes accessed | tf_op | source)
XLA Modules:
  0.0 163.3 jit_solution(18225060457859008187)
XLA Ops:
  0.7 1.4 gather_fusion
  2.1 0.7 broadcast_multiply_fusion
  2.8 11.6 %gather_fusion.1 = bf16[32,2,64,1536]{3,2,1,0:T(8,128)(2,1)} fusion(bf16[32,2,64,1536]{3,2,1,0:T(8,128)(2,1)} %param.7, s32[1024]{0:T(1024)S(1)} %pad_clamp_fusion.1), kind=kCustom, calls=%fused_computation.1 | custom fusion | bytes 25165952 | tf_op jit(solution)/shard_map/jit(_take)/gather | solution.py:135
  14.3 6.5 %bitcast_select_fusion = bf16[32,128,1536]{2,1,0:T(8,128)(2,1)S(1)} fusion(bf16[32,2,64,1536]{3,2,1,0:T(8,128)(2,1)} %gather_fusion.1, pred[32]{0:T(512)(128)(4,1)S(1)} %get-tuple-element.33), kind=kLoop, calls=%fused_computation.6 | loop fusion | flops 6291456 | bytes 25165856 | tf_op jit(solution)/shard_map/jit(_take)/select_n | solution.py:135
  20.9 4.8 %fusion = f32[32,128,128]{2,1,0:T(8,128)} fusion(bf16[32,128,1536]{2,1,0:T(8,128)(2,1)S(1)} %bitcast_select_fusion, f32[1536]{0:T(1024)S(1)} %broadcast_multiply_fusion), kind=kOutput, calls=%fused_computation.4 | convolution fusion | flops 1629487104 | bytes 14686208 | tf_op jit(solution)/shard_map/nax,nbx->nab/dot_general | solution.py:108
  25.6 2.8 %fusion.9 = (f32[32,1,64,64]{3,2,0,1:T(8,128)S(1)}, f32[32,1,64,64]{3,2,0,1:T(8,128)S(1)}) fusion(f32[32,128,128]{2,1,0:T(8,128)} %fusion), kind=kLoop, calls=%fused_computation.22 | loop fusion | flops 262144 | bytes 3145728 | tf_op jit(solution)/shard_map/stack | solution.py:69
  28.9 2.3 %reshape.321 = f32[32,1,8192]{2,1,0:T(1,128)} reshape(f32[32,1,2,64,64]{4,3,2,1,0:T(8,128)S(1)} %copy.45) | data formatting | bytes 2097152
  31.1 8.6 %all-to-all-start = ((f32[32,1,8192]{2,1,0:T(1,128)}), f32[32,1,8192]{2,1,0:T(1,128)S(1)}, u32[]{:S(2)}, u32[]{:S(2)}) async-start(f32[32,1,8192]{2,1,0:T(1,128)} %reshape.321), calls=%async_computation | async-start | bytes 2097152 | tf_op jit(solution)/shard_map/all_to_all | solution.py:23
  41.7 1.6 sort.17
  44.0 0.7 dynamic-slice.5
  44.6 0.7 compare_convert_fusion
  45.3 11.5 %all-to-all-done = f32[32,1,8192]{2,1,0:T(1,128)S(1)} async-done(((f32[32,1,8192]{2,1,0:T(1,128)}), f32[32,1,8192]{2,1,0:T(1,128)S(1)}, u32[]{:S(2)}, u32[]{:S(2)}) %all-to-all-start) | async-done | bytes 1048608 | tf_op jit(solution)/shard_map/all_to_all | solution.py:23
  57.3 3.2 %reduce.10 = f32[32,8192]{1,0:T(8,128)S(1)} reduce(f32[32,1,8192]{2,1,0:T(1,128)S(1)} %all-to-all-done, f32[]{:T(128)} %broadcast.237), dimensions={1}, to_apply=%all_to_all.6.reduce_sub_computation | reduce | bytes 2097156 | tf_op jit(solution)/shard_map/all_to_all | solution.py:23
  60.5 0.8 reshape.322
  63.7 5.8 %custom-call.10 = f32[1,64,64]{2,1,0:T(8,128)S(1)} custom-call(f32[1,64,64]{2,1,0:T(8,128)S(1)} %fusion.22), custom_call_target="Cholesky" | custom-call | tf_op jit(solution)/shard_map/vmap(jit(cholesky))/cholesky | solution.py:79
  70.8 4.9 %custom-call.11 = f32[1,1,64,64]{2,3,1,0:T(8,128)S(1)} custom-call(f32[1,1,64,64]{3,2,1,0:T(8,128)S(1)} %fusion.13), custom_call_target="InvertDiagBlocksLowerTriangular" | custom-call | tf_op jit(solution)/shard_map/vmap()/triangular_solve/custom-call.0 | solution.py:80
  76.6 5.8 %custom-call.12 = f32[1,64,64]{2,1,0:T(8,128)S(1)} custom-call(f32[1,64,64]{2,1,0:T(8,128)S(1)} %fusion.20), custom_call_target="Cholesky" | custom-call | tf_op jit(solution)/shard_map/vmap(jit(cholesky))/cholesky | solution.py:79
  83.1 0.7 fusion.14
  83.8 4.9 %custom-call.13 = f32[1,1,64,64]{2,3,1,0:T(8,128)S(1)} custom-call(f32[1,1,64,64]{3,2,1,0:T(8,128)S(1)} %fusion.14), custom_call_target="InvertDiagBlocksLowerTriangular" | custom-call | tf_op jit(solution)/shard_map/vmap()/triangular_solve/custom-call.0 | solution.py:80
  89.6 5.8 %custom-call.14 = f32[1,64,64]{2,1,0:T(8,128)S(1)} custom-call(f32[1,64,64]{2,1,0:T(8,128)S(1)} %fusion.18), custom_call_target="Cholesky" | custom-call | tf_op jit(solution)/shard_map/vmap(jit(cholesky))/cholesky | solution.py:79
  96.1 0.7 fusion.15
  96.7 4.9 %custom-call.15 = f32[1,1,64,64]{2,3,1,0:T(8,128)S(1)} custom-call(f32[1,1,64,64]{3,2,1,0:T(8,128)S(1)} %fusion.15), custom_call_target="InvertDiagBlocksLowerTriangular" | custom-call | tf_op jit(solution)/shard_map/vmap()/triangular_solve/custom-call.0 | solution.py:80
  102.1 1.2 broadcast_in_dim.65
  103.3 3.9 %all-to-all-start.1 = ((bf16[32,1,128,128]{3,2,1,0:T(8,128)(2,1)}), bf16[32,1,128,128]{3,2,1,0:T(8,128)(2,1)S(1)}, u32[]{:S(2)}, u32[]{:S(2)}) async-start(bf16[32,1,128,128]{3,2,1,0:T(8,128)(2,1)} %broadcast_in_dim.65), calls=%async_computation.1 | async-start | bytes 2097152 | tf_op jit(solution)/shard_map/all_to_all | solution.py:39
  107.7 0.7 compare_select_fusion.5
  108.4 11.7 %psum.28 = f32[64]{0:T(128)S(1)} all-reduce(f32[64]{0:T(128)S(1)} %compare_select_fusion.5), channel_id=1, replica_groups=mesh['space_0'=4,'space_1'=4,'space_2'=2,'freq'=4] {'space_0'}, use_global_device_ids=true, to_apply=%region_6.9 | all-reduce | flops 64 | bytes 512 | tf_op jit(solution)/shard_map/psum | solution.py:49
  120.1 14.8 %psum.29 = f32[64]{0:T(128)S(1)} all-reduce(f32[64]{0:T(128)S(1)} %psum.28), channel_id=1, replica_groups=mesh['space_0'=4,'space_1'=4,'space_2'=2,'freq'=4] {'space_1'}, use_global_device_ids=true, to_apply=%region_7.10 | all-reduce | flops 64 | bytes 512 | tf_op jit(solution)/shard_map/psum | solution.py:49
  134.9 2.5 %psum.30 = f32[64]{0:T(128)S(1)} all-reduce(f32[64]{0:T(128)S(1)} %psum.29), channel_id=1, replica_groups=mesh['space_0'=4,'space_1'=4,'space_2'=2,'freq'=4] {'space_2'}, use_global_device_ids=true, to_apply=%region_8.11 | all-reduce | flops 64 | bytes 512 | tf_op jit(solution)/shard_map/psum | solution.py:49
  137.3 10.7 %psum.31 = f32[64]{0:T(128)S(1)} all-reduce(f32[64]{0:T(128)S(1)} %psum.30), channel_id=1, replica_groups=mesh['space_0'=4,'space_1'=4,'space_2'=2,'freq'=4] {'freq'}, use_global_device_ids=true, to_apply=%region_9.12 | all-reduce | flops 64 | bytes 512 | tf_op jit(solution)/shard_map/psum | solution.py:49
  148.0 1.2 compare_select_fusion.4
  149.7 0.7 gather_fusion.2
  150.5 12.8 %convolution_convert_fusion = bf16[32,128,1536]{2,1,0:T(8,128)(2,1)} fusion(bf16[32,128,1536]{2,1,0:T(8,128)(2,1)} %bitcast.148, bf16[32,128,128]{2,1,0:T(8,128)(2,1)S(1)} %gather_fusion.2, pred[32]{0:T(512)(128)(4,1)S(1)} %compare_and_fusion.1), kind=kOutput, calls=%fused_computation.5 | convolution fusion | flops 1617428480 | bytes 26214432 | tf_op jit(solution)/shard_map/nmb,nbx->nmx/dot_general | solution.py:146
  (50 shorter events, 8.8 us)
Async XLA Ops:
  25.6 14.2 %copy-start = (s32[128]{0:T(128)S(1)}, s32[128]{0:T(128)}, u32[]{:S(2)}) copy-start(s32[128]{0:T(128)} %param.10) | copy-start | bytes 1540
  25.6 18.3 %copy-start.1 = (s32[128]{0:T(128)S(1)}, s32[128]{0:T(128)}, u32[]{:S(2)}) copy-start(s32[128]{0:T(128)} %param.9) | copy-start | bytes 1540
  31.1 25.7 %all-to-all-start = ((f32[32,1,8192]{2,1,0:T(1,128)}), f32[32,1,8192]{2,1,0:T(1,128)S(1)}, u32[]{:S(2)}, u32[]{:S(2)}) async-start(f32[32,1,8192]{2,1,0:T(1,128)} %reshape.321), calls=%async_computation | async-start | bytes 2097152 | tf_op jit(solution)/shard_map/all_to_all | solution.py:23
  103.3 46.4 %all-to-all-start.1 = ((bf16[32,1,128,128]{3,2,1,0:T(8,128)(2,1)}), bf16[32,1,128,128]{3,2,1,0:T(8,128)(2,1)S(1)}, u32[]{:S(2)}, u32[]{:S(2)}) async-start(bf16[32,1,128,128]{3,2,1,0:T(8,128)(2,1)} %broadcast_in_dim.65), calls=%async_computation.1 | async-start | bytes 2097152 | tf_op jit(solution)/shard_map/all_to_all | solution.py:39
where the time goes:
time: 164 us; the launch traced here: 163 us
  other arithmetic  55.5 us (34%)
  blocking collectives  39.6 us (24%)
  local copies, waits for them, and re-layouts  20.4 us (12%)
  matrix products  20.2 us (12%)
  starting transfers between devices  12.6 us (8%)
  waiting for transfers between devices  11.5 us (7%)
  between operations  3.59 us (2%)
    psum x4, blocking collectives, by_axis(): return functools.reduce(lax.psum, axes, shard)  39.6 us
    another operation x9, other arithmetic, iterate(): lower_tri = jnp.linalg.cholesky(gram_mat)  19.6 us
    another operation x6, other arithmetic, iterate(): lax.linalg.triangular_solve(lower_tri, image_cols, left_side=False, lower...  16.6 us
    dot_general x1, matrix products, shards(): jnp.einsum('nmb,nbx->nmx', own_bases, flat_rows, preferred_element_type=j...  12.8 us
    gather x1, local copies, waits for them, and re-layouts, shards(): grams = weighted_grams(jnp.take(coeffs, rows_send, axis=0), cell_weights)  11.6 us
    all_to_all x1, waiting for transfers between devices, sum_at_owner(): lax.all_to_all(parts, axis, split_axis=0, concat_axis=0, tiled=True)  11.5 us
    all_to_all x1, starting transfers between devices, sum_at_owner(): lax.all_to_all(parts, axis, split_axis=0, concat_axis=0, tiled=True)  8.62 us
    select_n x2, other arithmetic, shards(): grams = weighted_grams(jnp.take(coeffs, rows_send, axis=0), cell_weights)  6.54 us
  transfers between devices with their start and end apart: 2, of which 1 were waited for; matrix products, arithmetic and copies ran while one was open for 4% of the time, Pallas kernels for 0%

commit v1 on v0

v1 whole, which is shorter than its diff:
```python
import functools

import jax
import jax.numpy as jnp
from jax import lax
from jax.experimental import pallas as pl
from jax.experimental.pallas import tpu as pltpu
from jax.sharding import Mesh
from jax.sharding import PartitionSpec as P

M = 64
SPACE = ("space_0", "space_1", "space_2")
PLANE = ("space_0", "space_1")
CORE = "space_2"
SPACE_FREQ = ("space_0", "space_1", "space_2", "freq")
HIGH = lax.Precision.HIGHEST
BLK = 16
PAY = 80

VMEM_SPEC = pl.BlockSpec(memory_space=pltpu.VMEM)
SMEM_SPEC = pl.BlockSpec(memory_space=pltpu.SMEM)
ANY_SPEC = pl.BlockSpec(memory_space=pl.ANY)


def nt(a, b, precision=None):
    return lax.dot_general(
        a, b, (((1,), (1,)), ((), ())), precision=precision, preferred_element_type=jnp.float32
    )


def nn(a, b, precision=None):
    return lax.dot_general(
        a, b, (((1,), (0,)), ((), ())), precision=precision, preferred_element_type=jnp.float32
    )


def iotas(shape):
    return (
        lax.broadcasted_iota(jnp.int32, shape, 0),
        lax.broadcasted_iota(jnp.int32, shape, 1),
    )


def place_of(i, half, where, order):
    core = where[1] if half == 1 else 1 - where[1]
    return order[(2 * i + core) * where[3] + where[0]] - where[0] * where[2]


def fold_pack(prod):
    sym = prod + prod.T
    top = sym[:64]
    bot = pltpu.roll(sym[64:], 64, 1)
    _, lane = iotas((64, 128))
    both = 0.5 * jnp.where(lane < 64, top + bot, top - bot)
    row, lane = iotas((32, 128))
    up, low = both[:32], both[32:]
    left = pltpu.roll(low, 96, 1)
    right = pltpu.roll(low, 32, 1)
    out = jnp.where((lane < 32) & (lane < row), left, up)
    inner = (lane >= 64) & (lane < 96)
    out = jnp.where(inner & (lane - 64 < row), left, out)
    return jnp.where(inner & (lane - 64 == row), right, out)


def unpack(packed):
    row, lane = iotas((32, 128))
    turned = jnp.concatenate([packed, jnp.zeros((96, 128), jnp.float32)], axis=0).T
    t0, t1, t2, t3 = (turned[32 * k : 32 * k + 32] for k in range(4))
    t2 = pltpu.roll(t2, 64, 1)
    t3 = pltpu.roll(t3, 64, 1)
    inner = lane - 64
    cr00 = jnp.where(lane >= row, packed, t0)
    ci00 = jnp.where(inner > row, packed, jnp.where(inner == row, 0.0, -t2))
    upper = jnp.where(lane < 32, cr00, jnp.where((lane >= 64) & (lane < 96), ci00, packed))
    diag = pltpu.roll(packed, 64, 1)
    cr11 = jnp.where(lane < row, packed, jnp.where(lane == row, diag, t0))
    ci11 = jnp.where(inner < row, packed, jnp.where(inner == row, 0.0, -t2))
    both11 = pltpu.roll(jnp.where(lane < 64, cr11, ci11), 32, 1)
    ends = jnp.where(lane < 64, t1, -t3)
    second = ((lane >= 32) & (lane < 64)) | (lane >= 96)
    lower = jnp.where(second, both11, ends)
    return jnp.concatenate([upper, lower], axis=0)


def gram_kernel(where, order, cells_ref, coeffs, send_ref, own_ref, kept_ref, prods, sems):
    count = send_ref.shape[0]

    def copy(i, half):
        k = i + half * count
        src = coeffs.at[place_of(i, half, where, order)]
        return pltpu.make_async_copy(src, kept_ref.at[k], sems.at[k])

    for half in (0, 1):

        @pl.loop(0, count)
        def _(i, half=half):
            copy(i, half).start()

    cells = cells_ref[...].reshape(1, -1) / where[5].astype(jnp.float32)
    for half, out_ref in ((0, send_ref), (1, own_ref)):

        @pl.loop(0, count)
        def _(i, half=half):
            copy(i, half).wait()
            k = i + half * count
            rows = kept_ref[k]
            weighted = (rows.astype(jnp.float32) * cells).astype(jnp.bfloat16)
            prods[i] = nt(rows, weighted)

        @pl.loop(0, count, step=4)
        def _(i, out_ref=out_ref):
            for j in range(4):
                out_ref[i + j] = fold_pack(prods[i + j])


def orth_rows(zt, floor=0.0):
    n = zt.shape[0]
    gram = nt(zt, zt, HIGH)
    rest_g, rest_z = gram, zt
    row, _ = iotas((BLK, 128))
    outs = []
    for blk in range(n // BLK):
        r0 = BLK * blk
        head_g, head_z = rest_g[:BLK], rest_z[:BLK]
        tail_g, tail_z = rest_g[BLK:], rest_z[BLK:]
        more = tail_g.shape[0]
        cols = [
            jnp.broadcast_to(head_g[:, r0 + j : r0 + j + 1], (BLK, 128)) for j in range(BLK)
        ]
        tails = [
            jnp.broadcast_to(tail_g[:, r0 + j : r0 + j + 1], (more, 128)) if more else None
            for j in range(BLK)
        ]
        acc = jnp.zeros((BLK, 128), jnp.float32)
        for j in range(BLK):
            here = row == j
            pivot = jnp.broadcast_to(cols[j][j : j + 1], (BLK, 128))
            if floor:
                pivot = jnp.maximum(pivot, floor)
            acc = jnp.where(here, head_z * lax.rsqrt(pivot), acc)
            inv = 1.0 / pivot

            def eliminated(x, j=j, here=here, inv=inv, width=128):
                lead = jnp.broadcast_to(x[j : j + 1], x.shape) * inv[:, :width]
                return jnp.where(here[:, :width], lead, x - cols[j][:, :width] * lead)

            head_z = eliminated(head_z)
            if more:
                head_g = eliminated(head_g, width=n)
            for jj in range(j + 1, BLK):
                cols[jj] = eliminated(cols[jj])
        outs.append(acc)
        for j in range(BLK if more else 0):
            tail_z = tail_z - tails[j] * head_z[j : j + 1]
            tail_g = tail_g - tails[j][:, :n] * head_g[j : j + 1]
        rest_g, rest_z = tail_g, tail_z
    return jnp.concatenate(outs, axis=0)


def solve_kernel(where, order, counts, parts_ref, pay_ref, ritz_ref):
    summed = parts_ref[0]
    for i in range(1, parts_ref.shape[0]):
        summed = summed + parts_ref[i]
    both = unpack(summed)
    row, lane = iotas((64, 128))
    shift = jnp.sum(jnp.where(row == lane, both, 0.0), keepdims=True) * (1.0 / 64.0)
    hermit = jnp.concatenate([jnp.where(lane < 64, both, -both), pltpu.roll(both, 64, 1)], axis=0)
    row, lane = iotas((128, 128))
    shifted = hermit * (1.0 / shift) + jnp.where(row == lane, 1.0, 0.0)
    basis = orth_rows(nn(shifted[:64], shifted, HIGH), 0.25)
    basis = orth_rows(nn(basis, shifted, HIGH))
    quad = basis * nn(basis, hermit, HIGH)
    ritz = nt(jnp.ones((8, 128), jnp.float32), quad, HIGH)
    slot = where[4]
    kept = counts[order[slot]]
    _, lane = iotas((8, 64))
    ritz = jnp.where(lane < kept, ritz, 0.0)
    ritz_ref[...] = ritz[:1]
    row, _ = iotas((64, 128))
    sent = jnp.where(row < kept, basis, 0.0).astype(jnp.bfloat16)
    one = ritz.astype(jnp.bfloat16)
    left = ritz - one.astype(jnp.float32)
    two = left.astype(jnp.bfloat16)
    three = left - two.astype(jnp.float32)
    row, _ = iotas((8, 128))
    upper = jnp.concatenate([one.astype(jnp.float32), two.astype(jnp.float32)], axis=1)
    lower = jnp.concatenate([three, jnp.zeros_like(three)], axis=1)
    tail = jnp.where(row == 0, upper, jnp.where(row == 1, lower, 0.0))
    tail = jnp.concatenate([tail, jnp.zeros((8, 128), jnp.float32)], axis=0).astype(jnp.bfloat16)
    for i in range(pay_ref.shape[0]):
        pay_ref[i, :64] = sent
        pay_ref[i, 64:] = tail


def modes_kernel(half, where, order, bases_ref, kept_ref, *rest):
    out, expanders, stage, sems = rest[-4:]
    count = bases_ref.shape[0]
    slots = stage.shape[0]
    _, lane = iotas((64, 128))
    for i in range(count):
        basis = bases_ref[i, :64].astype(jnp.float32)
        expanders[i, :64] = jnp.where(lane < 64, basis, -basis).astype(jnp.bfloat16)
        expanders[i, 64:] = pltpu.roll(basis, 64, 1).astype(jnp.bfloat16)

    def copy(i):
        s = lax.rem(i, slots)
        return pltpu.make_async_copy(stage.at[s], out.at[place_of(i, half, where, order)], sems.at[s])

    @pl.loop(0, count)
    def _(i):
        @pl.when(i >= slots)
        def _():
            copy(i - slots).wait()

        stage[lax.rem(i, slots)] = nn(expanders[i], kept_ref[i + half * count]).astype(jnp.bfloat16)
        copy(i).start()

    for i in range(count - slots, count):
        copy(i).wait()


def compiler(mib):
    return pltpu.CompilerParams(vmem_limit_bytes=mib * 2**20)


def shards(coeffs, weights, mode_counts, owner_order):
    fgroup, _, blocks, points = coeffs.shape
    freqs = lax.axis_size("freq")
    group, core = lax.axis_index("freq"), lax.axis_index(CORE)
    space = lax.axis_index(SPACE)
    plane = lax.axis_size(PLANE)
    as32 = functools.partial(jnp.asarray, dtype=jnp.int32)
    where = jnp.stack(
        [as32(group), as32(core), as32(fgroup), as32(freqs), as32(space * freqs + group), as32(points * lax.axis_size(SPACE))]
    )
    rows = coeffs.reshape(fgroup, 2 * blocks, points)
    f32, bf16 = jnp.float32, jnp.bfloat16
    packed = jax.ShapeDtypeStruct((plane, 32, 128), f32)
    send, own, kept = pl.pallas_call(
        gram_kernel,
        out_shape=(packed, packed, pltpu.VMEM((fgroup, 2 * blocks, points), bf16)),
        in_specs=[SMEM_SPEC, SMEM_SPEC, VMEM_SPEC, ANY_SPEC],
        out_specs=(VMEM_SPEC, VMEM_SPEC, VMEM_SPEC),
        scratch_shapes=[
            pltpu.VMEM((plane, 128, 128), f32),
            pltpu.SemaphoreType.DMA((fgroup,)),
        ],
        compiler_params=compiler(32),
        name="gram",
    )(where, owner_order, weights, rows)
    swap = [(0, 1), (1, 0)]
    mine = own + lax.ppermute(send, CORE, swap)
    parts = lax.all_to_all(mine, PLANE, 0, 0, tiled=True)
    payload, ritz = pl.pallas_call(
        solve_kernel,
        out_shape=(
            jax.ShapeDtypeStruct((plane, PAY, 128), bf16),
            jax.ShapeDtypeStruct((1, M), f32),
        ),
        in_specs=[SMEM_SPEC, SMEM_SPEC, SMEM_SPEC, VMEM_SPEC],
        out_specs=(VMEM_SPEC, VMEM_SPEC),
        compiler_params=compiler(16),
        name="solve",
    )(where, owner_order, mode_counts, parts)
    bases = lax.all_to_all(payload, PLANE, 0, 0, tiled=True)
    others = lax.ppermute(bases, CORE, swap)

    def total(b):
        tail = b[:, 64:66].astype(f32).sum(axis=0)
        return tail[0, :64] + tail[0, 64:] + tail[1, :64]

    def modes(half, bases, *into):
        return pl.pallas_call(
            functools.partial(modes_kernel, half),
            out_shape=jax.ShapeDtypeStruct((fgroup, 2 * blocks, points), bf16),
            in_specs=[SMEM_SPEC, SMEM_SPEC, VMEM_SPEC, VMEM_SPEC] + [ANY_SPEC] * len(into),
            out_specs=ANY_SPEC,
            scratch_shapes=[
                pltpu.VMEM((plane, 128, 128), bf16),
                pltpu.VMEM((4, 2 * blocks, points), bf16),
                pltpu.SemaphoreType.DMA((4,)),
            ],
            input_output_aliases={4: 0} if into else {},
            compiler_params=compiler(16),
            name="modes%d" % half,
        )(where, owner_order, bases, kept, *into)

    fields = modes(1, bases)
    fields = modes(0, others, fields)
    energy = total(bases) + total(others)
    ring = [
        lax.ppermute(energy, "freq", [(i, (i + k) % freqs) for i in range(freqs)])
        for k in range(1, freqs)
    ]
    energy = functools.reduce(jnp.add, ring, energy) / (fgroup * freqs)
    return (fields.reshape(fgroup, 2, M, points), ritz, energy)


def solution(mesh):
    split = Mesh(
        mesh.devices.reshape(4, 4, 2, mesh.shape["freq"]), ("space_0", "space_1", "space_2", "freq")
    )
    placed = (P("freq", None, None, SPACE), P(SPACE), P(), P())
    return jax.shard_map(
        shards,
        mesh=split,
        in_specs=placed,
        out_specs=(P("freq", None, None, SPACE), P(SPACE_FREQ, None), P()),
        check_vma=False,
    )
```

time: 164 us -> 70 us (0.43)
  other arithmetic: 55.5 us -> 0.68 us
  Pallas kernels: 0 us -> 30.2 us
  matrix products: 20.2 us -> 0 us
  local copies, waits for them, and re-layouts: 20.4 us -> 1.44 us
  blocking collectives: 39.6 us -> 28.9 us
  waiting for transfers between devices: 11.5 us -> 3.13 us
  starting transfers between devices: 12.6 us -> 4.53 us
  between operations: 3.59 us -> 0.72 us
    psum x4 -> x0, blocking collectives: 39.6 us -> none  [by_axis(): return functools.reduce(lax.psum, axes, shard)]
    another operation x17 -> x0, other arithmetic: 39.1 us -> none  [the longest x9 19.6 us: iterate(): lower_tri = jnp.linalg.cholesky(gram_mat)]
    pallas_call x0 -> x4, Pallas kernels: none -> 30.2 us  [the longest x1 13.3 us: shards(): pl.pallas_call(gram_kernel, out_shape=(packed, packed, pltpu.VMEM((fgroup...]
    all_to_all x0 -> x2, blocking collectives: none -> 28.9 us  [the longest x1 16.9 us: shards(): parts = lax.all_to_all(mine, PLANE, 0, 0, tiled=True)]
    dot_general x9 -> x0, matrix products: 19.5 us -> none  [the longest x1 12.8 us: shards(): jnp.einsum('nmb,nbx->nmx', own_bases, flat_rows, preferred_element_type=j...]
    gather x5 -> x0, local copies, waits for them, and re-layouts: 14.9 us -> none  [the longest x1 11.6 us: shards(): grams = weighted_grams(jnp.take(coeffs, rows_send, axis=0), cell_weights)]
    all_to_all x2 -> x0, starting transfers between devices: 12.6 us -> none  [the longest x1 8.62 us: sum_at_owner(): lax.all_to_all(parts, axis, split_axis=0, concat_axis=0, tiled=True)]
    all_to_all x2 -> x0, waiting for transfers between devices: 11.5 us -> none  [the longest x1 11.5 us: sum_at_owner(): lax.all_to_all(parts, axis, split_axis=0, concat_axis=0, tiled=True)]
  transfers between devices with their start and end apart: 2 -> 5, of which waited for: 1 -> 2; matrix products, arithmetic and copies ran while one was open for 4% -> 0% of each run, Pallas kernels for 0% -> 16%
where the time goes in v1:
time: 70 us; the launch traced here: 69.6 us
  Pallas kernels  30.2 us (43%)
  blocking collectives  28.9 us (41%)
  starting transfers between devices  4.53 us (6%)
  waiting for transfers between devices  3.13 us (4%)
  local copies, waits for them, and re-layouts  1.44 us (2%)
  between operations  0.72 us (1%)
    all_to_all x1, blocking collectives, shards(): parts = lax.all_to_all(mine, PLANE, 0, 0, tiled=True)  16.9 us
    pallas_call x1, Pallas kernels, shards(): pl.pallas_call(gram_kernel, out_shape=(packed, packed, pltpu.VMEM((fgroup...  13.3 us
    all_to_all x1, blocking collectives, shards(): bases = lax.all_to_all(payload, PLANE, 0, 0, tiled=True)  11.9 us
    pallas_call x2, Pallas kernels, modes(): pl.pallas_call(functools.partial(modes_kernel, half), out_shape=jax.Shape...  11 us
    pallas_call x1, Pallas kernels, shards(): pl.pallas_call(solve_kernel, out_shape=(jax.ShapeDtypeStruct((plane, PAY,...  5.87 us
    ppermute x3, starting transfers between devices, shards(): lax.ppermute(energy, 'freq', [(i, (i + k) % freqs) for i in range(freqs)])  4.44 us
    ppermute x1, waiting for transfers between devices, shards(): others = lax.ppermute(bases, CORE, swap)  1.6 us
    ppermute x1, waiting for transfers between devices, shards(): mine = own + lax.ppermute(send, CORE, swap)  1.52 us
  transfers between devices with their start and end apart: 5, of which 2 were waited for; matrix products, arithmetic and copies ran while one was open for 0% of the time, Pallas kernels for 16%

profile of v1, /device:TPU:0, one launch (start us, length us, event | category | flops | bytes accessed | tf_op | source)
XLA Modules:
  0.0 69.6 jit_solution(16891840344916024510)
XLA Ops:
  0.6 0.0 copy-start.2
  0.7 0.1 stack.15.where
  0.7 0.0 copy-start
  0.7 0.7 %copy-done = f32[1536]{0:T(1024)S(1)} copy-done((f32[1536]{0:T(1024)S(1)}, f32[1536]{0:T(1024)}, u32[]{:S(2)}) %copy-start) | copy-done | bytes 6168
  1.4 0.0 copy-start.1
  1.4 0.7 copy-done.1
  2.1 13.3 %gram.1 = (f32[16,32,128]{2,1,0:T(8,128)S(1)}, f32[16,32,128]{2,1,0:T(8,128)S(1)}, bf16[32,128,1536]{2,1,0:T(8,128)(2,1)S(1)}) custom-call(s32[6]{0:T(128)S(1)} %stack.15.where, s32[128]{0:T(128)S(1)} %copy-done.1, f32[1536]{0:T(1024)S(1)} %copy-done, bf16[32,128,1536]{2,1,0:T(8,128)(2,1)} %bitcast.8), custom_call_target="tpu_custom_call" | custom-call | tf_op jit(solution)/shard_map/gram/pallas_call | solution.py:239
  15.4 0.1 collective-permute-start
  15.5 1.5 %collective-permute-done = f32[16,32,128]{2,1,0:T(8,128)S(1)} collective-permute-done((f32[16,32,128]{2,1,0:T(8,128)S(1)}, f32[16,32,128]{2,1,0:T(8,128)S(1)}, u32[]{:S(2)}, u32[]{:S(2)}) %collective-permute-start) | collective-permute-done | bytes 262176 | tf_op jit(solution)/shard_map/ppermute | solution.py:252
  17.1 16.9 %all_to_all.10.parts_ref = f32[16,32,128]{2,1,0:T(8,128)S(1)} all-to-all(f32[16,32,128]{2,1,0:T(8,128)S(1)} %add.46), channel_id=1, replica_groups=mesh['space_0'=4,'space_1'=4,'space_2'=2,'freq'=4] {'space_0','space_1'}, dimensions={0} | all-to-all | bytes 524288 | tf_op jit(solution)/shard_map/all_to_all | solution.py:253
  34.0 0.0 copy-done.2
  34.0 5.9 %solve.1 = (bf16[16,80,128]{2,1,0:T(8,128)(2,1)S(1)}, f32[1,64]{1,0:T(1,128)}) custom-call(s32[6]{0:T(128)S(1)} %stack.15.where, s32[128]{0:T(128)S(1)} %copy-done.1, s32[128]{0:T(128)S(1)} %copy-done.2, f32[16,32,128]{2,1,0:T(8,128)S(1)} %all_to_all.10.parts_ref), custom_call_target="tpu_custom_call" | custom-call | tf_op jit(solution)/shard_map/solve/pallas_call | solution.py:254
  39.9 11.9 %all_to_all.11.bases_ref = bf16[16,80,128]{2,1,0:T(8,128)(2,1)S(1)} all-to-all(bf16[16,80,128]{2,1,0:T(8,128)(2,1)S(1)} %get-tuple-element.10), channel_id=1, replica_groups=mesh['space_0'=4,'space_1'=4,'space_2'=2,'freq'=4] {'space_0','space_1'}, dimensions={0} | all-to-all | bytes 655360 | tf_op jit(solution)/shard_map/all_to_all | solution.py:265
  51.8 0.0 collective-permute-start.1
  51.9 1.6 %collective-permute-done.1.bases_ref = bf16[16,80,128]{2,1,0:T(8,128)(2,1)S(1)} collective-permute-done((bf16[16,80,128]{2,1,0:T(8,128)(2,1)S(1)}, bf16[16,80,128]{2,1,0:T(8,128)(2,1)S(1)}, u32[]{:S(2)}, u32[]{:S(2)}) %collective-permute-start.1) | collective-permute-done | bytes 327712 | tf_op jit(solution)/shard_map/ppermute | solution.py:266
  53.5 0.1 add_bitcast_fusion
  53.6 2.8 %collective-permute-start.4 = (f32[64]{0:T(128)S(1)}, f32[64]{0:T(128)S(1)}, u32[]{:S(2)}, u32[]{:S(2)}) collective-permute-start(f32[64]{0:T(128)S(1)} %add_bitcast_fusion), channel_id=1, source_target_pairs={{0,3},{1,0},{2,1},{3,2},{4,7},{5,4},{6,5},{7,6},{8,11},{9,8},{10,9... | collective-permute-start | bytes 776 | tf_op jit(solution)/shard_map/ppermute | solution.py:292
  56.3 0.8 %collective-permute-start.3 = (f32[64]{0:T(128)S(1)}, f32[64]{0:T(128)S(1)}, u32[]{:S(2)}, u32[]{:S(2)}) collective-permute-start(f32[64]{0:T(128)S(1)} %add_bitcast_fusion), channel_id=1, source_target_pairs={{0,2},{1,3},{2,0},{3,1},{4,6},{5,7},{6,4},{7,5},{8,10},{9,11},{10,... | collective-permute-start | bytes 776 | tf_op jit(solution)/shard_map/ppermute | solution.py:292
  57.1 0.9 %collective-permute-start.2 = (f32[64]{0:T(128)S(1)}, f32[64]{0:T(128)S(1)}, u32[]{:S(2)}, u32[]{:S(2)}) collective-permute-start(f32[64]{0:T(128)S(1)} %add_bitcast_fusion), channel_id=1, source_target_pairs={{0,1},{1,2},{2,3},{3,0},{4,5},{5,6},{6,7},{7,4},{8,9},{9,10},{10,1... | collective-permute-start | bytes 776 | tf_op jit(solution)/shard_map/ppermute | solution.py:292
  58.0 5.5 %modes1.1.rest_0_ = bf16[32,128,1536]{2,1,0:T(8,128)(2,1)} custom-call(s32[6]{0:T(128)S(1)} %stack.15.where, s32[128]{0:T(128)S(1)} %copy-done.1, bf16[16,80,128]{2,1,0:T(8,128)(2,1)S(1)} %all_to_all.11.bases_ref, bf16[32,128,1536]{2,1,0:T(8,128)(2,1)S(1)} %get-tuple-element.11.kept_ref), custom_call_target="tpu_custom_call" | custom-call | tf_op jit(solution)/shard_map/modes1/pallas_call | solution.py:273
  63.5 5.5 %modes0.1 = bf16[32,128,1536]{2,1,0:T(8,128)(2,1)} custom-call(s32[6]{0:T(128)S(1)} %stack.15.where, s32[128]{0:T(128)S(1)} %copy-done.1, bf16[16,80,128]{2,1,0:T(8,128)(2,1)S(1)} %collective-permute-done.1.bases_ref, bf16[32,128,1536]{2,1,0:T(8,128)(2,1)S(1)} %get-tuple-element.11.kept_ref, ...), custom_call_target="tpu_custom_call", output_to_operand_aliasing={{}: (4, {})} | custom-call | tf_op jit(solution)/shard_map/modes0/pallas_call | solution.py:273
  69.1 0.0 collective-permute-done.4
  69.1 0.0 collective-permute-done.3
  69.1 0.0 collective-permute-done.2
  69.1 0.5 add_multiply_fusion
  (3 shorter events, 0.1 us)
Async XLA Ops:
  0.6 33.4 %copy-start.2 = (s32[128]{0:T(128)S(1)}, s32[128]{0:T(128)}, u32[]{:S(2)}) copy-start(s32[128]{0:T(128)} %counts.1) | copy-start | bytes 1540
  0.7 0.7 %copy-start = (f32[1536]{0:T(1024)S(1)}, f32[1536]{0:T(1024)}, u32[]{:S(2)}) copy-start(f32[1536]{0:T(1024)} %cells_ref.1) | copy-start | bytes 18436
  1.4 0.7 copy-start.1
  15.4 1.6 %collective-permute-start = (f32[16,32,128]{2,1,0:T(8,128)S(1)}, f32[16,32,128]{2,1,0:T(8,128)S(1)}, u32[]{:S(2)}, u32[]{:S(2)}) collective-permute-start(f32[16,32,128]{2,1,0:T(8,128)S(1)} %get-tuple-element.9), channel_id=1, source_target_pairs={{0,4},{4,0},{1,5},{5,1},{2,6},{6,2},{3,7},{7,3},{8,12},{12,8},{9,1... | collective-permute-start | bytes 786440 | tf_op jit(solution)/shard_map/ppermute | solution.py:252
  51.8 1.6 %collective-permute-start.1 = (bf16[16,80,128]{2,1,0:T(8,128)(2,1)S(1)}, bf16[16,80,128]{2,1,0:T(8,128)(2,1)S(1)}, u32[]{:S(2)}, u32[]{:S(2)}) collective-permute-start(bf16[16,80,128]{2,1,0:T(8,128)(2,1)S(1)} %all_to_all.11.bases_ref), channel_id=1, source_target_pairs={{0,4},{4,0},{1,5},{5,1},{2,6},{6,2},{3,7},{7,3},{8,12},{12,8},{9,1... | collective-permute-start | bytes 983048 | tf_op jit(solution)/shard_map/ppermute | solution.py:266
  53.6 15.5 %collective-permute-start.4 = (f32[64]{0:T(128)S(1)}, f32[64]{0:T(128)S(1)}, u32[]{:S(2)}, u32[]{:S(2)}) collective-permute-start(f32[64]{0:T(128)S(1)} %add_bitcast_fusion), channel_id=1, source_target_pairs={{0,3},{1,0},{2,1},{3,2},{4,7},{5,4},{6,5},{7,6},{8,11},{9,8},{10,9... | collective-permute-start | bytes 776 | tf_op jit(solution)/shard_map/ppermute | solution.py:292
  56.3 12.7 %collective-permute-start.3 = (f32[64]{0:T(128)S(1)}, f32[64]{0:T(128)S(1)}, u32[]{:S(2)}, u32[]{:S(2)}) collective-permute-start(f32[64]{0:T(128)S(1)} %add_bitcast_fusion), channel_id=1, source_target_pairs={{0,2},{1,3},{2,0},{3,1},{4,6},{5,7},{6,4},{7,5},{8,10},{9,11},{10,... | collective-permute-start | bytes 776 | tf_op jit(solution)/shard_map/ppermute | solution.py:292
  57.1 11.9 %collective-permute-start.2 = (f32[64]{0:T(128)S(1)}, f32[64]{0:T(128)S(1)}, u32[]{:S(2)}, u32[]{:S(2)}) collective-permute-start(f32[64]{0:T(128)S(1)} %add_bitcast_fusion), channel_id=1, source_target_pairs={{0,1},{1,2},{2,3},{3,0},{4,5},{5,6},{6,7},{7,4},{8,9},{9,10},{10,1... | collective-permute-start | bytes 776 | tf_op jit(solution)/shard_map/ppermute | solution.py:292

commit v2 on v1

v2 whole, which is shorter than its diff:
```python
import functools

import jax
import jax.numpy as jnp
from jax import lax
from jax.experimental import pallas as pl
from jax.experimental.pallas import tpu as pltpu
from jax.sharding import Mesh
from jax.sharding import PartitionSpec as P

M = 64
ITERS = 3
SPACE = ("space_0", "space_1", "space_2")
PLANE = ("space_0", "space_1")
CORE = "space_2"
SPACE_FREQ = ("space_0", "space_1", "space_2", "freq")
HIGH = lax.Precision.HIGHEST
BLK = 16
PAY = 80
UNROLL = 4
FLIGHT = 4

VMEM_SPEC = pl.BlockSpec(memory_space=pltpu.VMEM)
ANY_SPEC = pl.BlockSpec(memory_space=pl.ANY)
SMEM_SPEC = pl.BlockSpec(memory_space=pltpu.SMEM)
HBM_SPEC = pl.BlockSpec(memory_space=pltpu.HBM)


def nt(a, b, precision=None):
    return lax.dot_general(
        a, b, (((1,), (1,)), ((), ())), precision=precision, preferred_element_type=jnp.float32
    )


def nn(a, b, precision=None):
    return lax.dot_general(
        a, b, (((1,), (0,)), ((), ())), precision=precision, preferred_element_type=jnp.float32
    )


def iotas(shape):
    return (
        lax.broadcasted_iota(jnp.int32, shape, 0),
        lax.broadcasted_iota(jnp.int32, shape, 1),
    )


def here():
    group, core = lax.axis_index("freq"), lax.axis_index(CORE)
    plane = lax.axis_index(PLANE[0]) * lax.axis_size(PLANE[1]) + lax.axis_index(PLANE[1])
    return group, core, plane


def slot_of(plane, core, group):
    return (plane * lax.axis_size(CORE) + core) * lax.axis_size("freq") + group


def place_of(i, half, order, per_group):
    group, core, _ = here()
    return order[slot_of(i, core if half == 1 else 1 - core, group)] - group * per_group


def fold_pack(prod):
    sym = prod + prod.T
    top = sym[:64]
    bot = pltpu.roll(sym[64:], 64, 1)
    _, lane = iotas((64, 128))
    both = 0.5 * jnp.where(lane < 64, top + bot, top - bot)
    row, lane = iotas((32, 128))
    up, low = both[:32], both[32:]
    left = pltpu.roll(low, 96, 1)
    right = pltpu.roll(low, 32, 1)
    out = jnp.where((lane < 32) & (lane < row), left, up)
    inner = (lane >= 64) & (lane < 96)
    out = jnp.where(inner & (lane - 64 < row), left, out)
    return jnp.where(inner & (lane - 64 == row), right, out)


def unpack(packed):
    row, lane = iotas((32, 128))
    turned = jnp.concatenate([packed, jnp.zeros((96, 128), jnp.float32)], axis=0).T
    t0, t1, t2, t3 = (turned[32 * k : 32 * k + 32] for k in range(4))
    t2 = pltpu.roll(t2, 64, 1)
    t3 = pltpu.roll(t3, 64, 1)
    inner = lane - 64
    cr00 = jnp.where(lane >= row, packed, t0)
    ci00 = jnp.where(inner > row, packed, jnp.where(inner == row, 0.0, -t2))
    upper = jnp.where(lane < 32, cr00, jnp.where((lane >= 64) & (lane < 96), ci00, packed))
    diag = pltpu.roll(packed, 64, 1)
    cr11 = jnp.where(lane < row, packed, jnp.where(lane == row, diag, t0))
    ci11 = jnp.where(inner < row, packed, jnp.where(inner == row, 0.0, -t2))
    both11 = pltpu.roll(jnp.where(lane < 64, cr11, ci11), 32, 1)
    ends = jnp.where(lane < 64, t1, -t3)
    second = ((lane >= 32) & (lane < 64)) | (lane >= 96)
    lower = jnp.where(second, both11, ends)
    return jnp.concatenate([upper, lower], axis=0)


def gram_kernel(order_hbm, counts_hbm, cells_hbm, coeffs, *rest):
    send_ref, own_ref, kept_ref, order, counts, cells, wide, packs, even, odd, side, sems = rest
    count = kept_ref.shape[0]
    chunks = count // UNROLL

    def fetch(k):
        part = pl.ds(k * UNROLL, UNROLL)
        return pltpu.make_async_copy(coeffs.at[part], kept_ref.at[part], sems.at[k])

    take_order = pltpu.make_async_copy(order_hbm, order, side.at[0])
    take_cells = pltpu.make_async_copy(cells_hbm, cells, side.at[1])
    take_counts = pltpu.make_async_copy(counts_hbm, counts, side.at[2])
    take_cells.start()
    for k in range(FLIGHT):
        fetch(k).start()
    take_order.start()
    take_counts.start()
    take_cells.wait()
    total = cells.shape[-1] * lax.axis_size(SPACE)
    wide[...] = jnp.broadcast_to(cells[...].reshape(1, -1) / total, wide.shape)

    def product(f):
        rows = kept_ref[f]
        scaled = rows.astype(jnp.float32).reshape(-1, *wide.shape) * wide[...]
        return nt(rows, scaled.reshape(rows.shape).astype(jnp.bfloat16))

    def arrived(k):
        fetch(k).wait()

        @pl.when(k + FLIGHT < chunks)
        def _():
            fetch(k + FLIGHT).start()

    def chunk(k, done, fill):
        for j in range(UNROLL):
            packs[(k - 1) * UNROLL + j] = fold_pack(done[j])
            fill[j] = product(k * UNROLL + j)

    arrived(0)
    for j in range(UNROLL):
        even[j] = product(j)

    @pl.loop(1, chunks - 1, step=2)
    def _(k):
        arrived(k)
        arrived(k + 1)
        chunk(k, even, odd)
        chunk(k + 1, odd, even)

    arrived(chunks - 1)
    chunk(chunks - 1, even, odd)
    for j in range(UNROLL):
        packs[count - UNROLL + j] = fold_pack(odd[j])
    take_order.wait()
    take_counts.wait()
    for half, out_ref in ((0, send_ref), (1, own_ref)):
        for i in range(count // 2):
            out_ref[i] = packs[place_of(i, half, order, count)]


def orth_rows(zt):
    n = zt.shape[0]
    gram = nt(zt, zt, HIGH)
    rest_g, rest_z = gram, zt
    row, _ = iotas((BLK, 128))
    outs = []
    for blk in range(n // BLK):
        r0 = BLK * blk
        head_g, head_z = rest_g[:BLK], rest_z[:BLK]
        more = n - r0 - BLK
        tail_g, tail_z = (rest_g[BLK:], rest_z[BLK:]) if more else (None, None)
        cols = [
            jnp.broadcast_to(head_g[:, r0 + j : r0 + j + 1], (BLK, 128)) for j in range(BLK)
        ]
        tails = [
            jnp.broadcast_to(tail_g[:, r0 + j : r0 + j + 1], (more, 128)) if more else None
            for j in range(BLK)
        ]
        acc = jnp.zeros((BLK, 128), jnp.float32)
        for j in range(BLK):
            here = row == j
            pivot = jnp.broadcast_to(cols[j][j : j + 1], (BLK, 128))
            acc = jnp.where(here, head_z * lax.rsqrt(pivot), acc)
            inv = 1.0 / pivot

            def eliminated(x, j=j, here=here, inv=inv, width=128):
                lead = jnp.broadcast_to(x[j : j + 1], x.shape) * inv[:, :width]
                return jnp.where(here[:, :width], lead, x - cols[j][:, :width] * lead)

            head_z = eliminated(head_z)
            if more:
                head_g = eliminated(head_g, width=n)
            for jj in range(j + 1, BLK):
                cols[jj] = eliminated(cols[jj])
        outs.append(acc)
        for j in range(BLK if more else 0):
            tail_z = tail_z - tails[j] * head_z[j : j + 1]
            tail_g = tail_g - tails[j][:, :n] * head_g[j : j + 1]
        rest_g, rest_z = tail_g, tail_z
    return jnp.concatenate(outs, axis=0)


def solve_kernel(order, counts, parts_ref, pay_ref, ritz_ref):
    summed = parts_ref[0]
    for i in range(1, parts_ref.shape[0]):
        summed = summed + parts_ref[i]
    both = unpack(summed)
    row, lane = iotas((64, 128))
    trace = jnp.sum(jnp.where(row == lane, both, 0.0)) * (1.0 / 64.0)
    shift = jnp.full((1, 1), trace)
    hermit = jnp.concatenate([jnp.where(lane < 64, both, -both), pltpu.roll(both, 64, 1)], axis=0)
    row, lane = iotas((128, 128))
    eye = jnp.where(row == lane, 1.0, 0.0)
    shifted = hermit * (1.0 / shift) + eye
    spread = jnp.sum(both * both) * 2.0
    mild = spread <= 512.0 * trace * trace
    start = jnp.where(mild, shifted[:64], eye[:64])
    sweeps = jnp.where(mild, ITERS - 1, ITERS)
    basis = lax.fori_loop(
        0, sweeps, lambda _, rows: orth_rows(nn(rows, shifted, HIGH)), start
    )
    quad = basis * nn(basis, hermit, HIGH)
    ritz = nt(jnp.ones((8, 128), jnp.float32), quad, HIGH)
    group, core, plane = here()
    kept = counts[order[slot_of(plane, core, group)]]
    _, lane = iotas((8, 64))
    ritz = jnp.where(lane < kept, ritz, 0.0)
    ritz_ref[...] = ritz[:1]
    row, _ = iotas((64, 128))
    sent = jnp.where(row < kept, basis, 0.0).astype(jnp.bfloat16)
    one = ritz.astype(jnp.bfloat16)
    left = ritz - one.astype(jnp.float32)
    two = left.astype(jnp.bfloat16)
    three = left - two.astype(jnp.float32)
    row, _ = iotas((8, 128))
    upper = jnp.concatenate([one.astype(jnp.float32), two.astype(jnp.float32)], axis=1)
    lower = jnp.concatenate([three, jnp.zeros_like(three)], axis=1)
    tail = jnp.where(row == 0, upper, jnp.where(row == 1, lower, 0.0))
    tail = jnp.concatenate([tail, jnp.zeros((8, 128), jnp.float32)], axis=0).astype(jnp.bfloat16)
    for i in range(pay_ref.shape[0]):
        pay_ref[i, :64] = sent
        pay_ref[i, 64:] = tail


def modes_kernel(order, own_ref, other_ref, kept_ref, out, expanders, stage, sems):
    count = kept_ref.shape[0]
    _, lane = iotas((64, 128))
    for half, bases_ref in ((1, own_ref), (0, other_ref)):
        for i in range(count // 2):
            k = i + (1 - half) * (count // 2)
            basis = bases_ref[i, :64].astype(jnp.float32)
            expanders[k, :64] = jnp.where(lane < 64, basis, -basis).astype(jnp.bfloat16)
            expanders[k, 64:] = pltpu.roll(basis, 64, 1).astype(jnp.bfloat16)
    group, core, _ = here()

    def place(k):
        far = lax.div(k, count // 2)
        i = k - far * (count // 2)
        return order[slot_of(i, core + far * (1 - 2 * core), group)] - group * count

    def copy(i):
        return pltpu.make_async_copy(stage.at[i], out.at[place(i)], sems.at[i])

    @pl.loop(0, count, step=UNROLL)
    def _(i):
        for j in range(UNROLL):
            rows = kept_ref[place(i + j)]
            stage[i + j] = nn(expanders[i + j], rows).astype(jnp.bfloat16)
            copy(i + j).start()

    @pl.loop(0, count)
    def _(i):
        copy(i).wait()


def compiler(mib):
    return pltpu.CompilerParams(vmem_limit_bytes=mib * 2**20)


def shards(coeffs, weights, mode_counts, owner_order):
    fgroup, _, blocks, points = coeffs.shape
    freqs = lax.axis_size("freq")
    plane = lax.axis_size(PLANE)
    slots = fgroup * freqs
    rows = coeffs.reshape(fgroup, 2 * blocks, points)
    f32, bf16 = jnp.float32, jnp.bfloat16
    packed = jax.ShapeDtypeStruct((plane, 32, 128), f32)
    in_hbm = [
        pltpu.with_memory_space_constraint(x, pltpu.HBM)
        for x in (owner_order, mode_counts, weights)
    ]
    send, own, kept, order, counts = pl.pallas_call(
        gram_kernel,
        out_shape=(
            packed,
            packed,
            pltpu.VMEM((fgroup, 2 * blocks, points), bf16),
            pltpu.SMEM((slots,), jnp.int32),
            pltpu.SMEM((slots,), jnp.int32),
        ),
        in_specs=[HBM_SPEC] * 4,
        out_specs=(VMEM_SPEC, VMEM_SPEC, VMEM_SPEC, SMEM_SPEC, SMEM_SPEC),
        scratch_shapes=[
            pltpu.VMEM((points,), f32),
            pltpu.VMEM((8, points), f32),
            pltpu.VMEM((fgroup, 32, 128), f32),
            pltpu.VMEM((UNROLL, 128, 128), f32),
            pltpu.VMEM((UNROLL, 128, 128), f32),
            pltpu.SemaphoreType.DMA((3,)),
            pltpu.SemaphoreType.DMA((fgroup // UNROLL,)),
        ],
        compiler_params=compiler(32),
        name="gram",
    )(*in_hbm, rows)
    swap = [(0, 1), (1, 0)]
    mine = own + lax.ppermute(send, CORE, swap)
    parts = lax.all_to_all(mine, PLANE, 0, 0, tiled=True)
    payload, ritz = pl.pallas_call(
        solve_kernel,
        out_shape=(pltpu.VMEM((plane, PAY, 128), bf16), pltpu.VMEM((1, M), f32)),
        in_specs=[SMEM_SPEC, SMEM_SPEC, VMEM_SPEC],
        out_specs=(VMEM_SPEC, VMEM_SPEC),
        compiler_params=compiler(16),
        name="solve",
    )(order, counts, parts)
    bases = lax.all_to_all(payload, PLANE, 0, 0, tiled=True)
    others = lax.ppermute(bases, CORE, swap)

    def total(b):
        tail = b[:, 64:66].astype(f32).sum(axis=0)
        return tail[0, :64] + tail[0, 64:] + tail[1, :64]

    fields = pl.pallas_call(
        modes_kernel,
        out_shape=jax.ShapeDtypeStruct((fgroup, 2 * blocks, points), bf16),
        in_specs=[SMEM_SPEC, VMEM_SPEC, VMEM_SPEC, VMEM_SPEC],
        out_specs=HBM_SPEC,
        scratch_shapes=[
            pltpu.VMEM((fgroup, 128, 128), bf16),
            pltpu.VMEM((fgroup, 2 * blocks, points), bf16),
            pltpu.SemaphoreType.DMA((fgroup,)),
        ],
        compiler_params=compiler(16),
        name="modes",
    )(order, bases, others, kept)
    energy = total(bases) + total(others)
    ring = [
        lax.ppermute(energy, "freq", [(i, (i + k) % freqs) for i in range(freqs)])
        for k in range(1, freqs)
    ]
    energy = functools.reduce(jnp.add, ring, energy) / (fgroup * freqs)
    return (fields.reshape(fgroup, 2, M, points), ritz, energy)


def solution(mesh):
    split = Mesh(
        mesh.devices.reshape(4, 4, 2, mesh.shape["freq"]), ("space_0", "space_1", "space_2", "freq")
    )
    placed = (P("freq", None, None, SPACE), P(SPACE), P(), P())
    return jax.shard_map(
        shards,
        mesh=split,
        in_specs=placed,
        out_specs=(P("freq", None, None, SPACE), P(SPACE_FREQ, None), P()),
        check_vma=False,
    )
```

time: 70 us -> 56.2 us (0.80)
  Pallas kernels: 30.2 us -> 17.4 us
  local copies, waits for them, and re-layouts: 1.44 us -> 0.51 us
    pallas_call x1, Pallas kernels: 13.3 us -> 6.67 us  [shards(): pl.pallas_call(gram_kernel, out_shape=(packed, packed, pltpu.VMEM((fgroup...]
    pallas_call x3 -> x2, Pallas kernels: 16.9 us -> 10.7 us  [the longest x1 5.82 us: shards(): pl.pallas_call(modes_kernel, out_shape=jax.ShapeDtypeStruct((fgroup, 2 *...]
    unnamed x6 -> x1, local copies, waits for them, and re-layouts: 1.36 us -> 0.51 us
  transfers between devices with their start and end apart: 5 -> 5, of which waited for: 2 -> 2; matrix products, arithmetic and copies ran while one was open for 0% -> 1% of each run, Pallas kernels for 16% -> 10%
where the time goes in v2:
time: 56.2 us; the launch traced here: 55.8 us
  blocking collectives  28.9 us (51%)
  Pallas kernels  17.4 us (31%)
  starting transfers between devices  4.54 us (8%)
  waiting for transfers between devices  3.13 us (6%)
  other arithmetic  0.69 us (1%)
  between operations  0.69 us (1%)
    all_to_all x1, blocking collectives, shards(): parts = lax.all_to_all(mine, PLANE, 0, 0, tiled=True)  16.9 us
    all_to_all x1, blocking collectives, shards(): bases = lax.all_to_all(payload, PLANE, 0, 0, tiled=True)  11.9 us
    pallas_call x1, Pallas kernels, shards(): pl.pallas_call(gram_kernel, out_shape=(packed, packed, pltpu.VMEM((fgroup...  6.67 us
    pallas_call x1, Pallas kernels, shards(): pl.pallas_call(modes_kernel, out_shape=jax.ShapeDtypeStruct((fgroup, 2 *...  5.82 us
    pallas_call x1, Pallas kernels, shards(): pl.pallas_call(solve_kernel, out_shape=(pltpu.VMEM((plane, PAY, 128), bf1...  4.91 us
    ppermute x3, starting transfers between devices, shards(): lax.ppermute(energy, 'freq', [(i, (i + k) % freqs) for i in range(freqs)])  4.45 us
    ppermute x1, waiting for transfers between devices, shards(): others = lax.ppermute(bases, CORE, swap)  1.6 us
    ppermute x1, waiting for transfers between devices, shards(): mine = own + lax.ppermute(send, CORE, swap)  1.52 us
  transfers between devices with their start and end apart: 5, of which 2 were waited for; matrix products, arithmetic and copies ran while one was open for 1% of the time, Pallas kernels for 10%

profile of v2, /device:TPU:0, one launch (start us, length us, event | category | flops | bytes accessed | tf_op | source)
XLA Modules:
  0.0 55.8 jit_solution(614741390056214215)
XLA Ops:
  0.6 6.7 %gram.1 = (f32[16,32,128]{2,1,0:T(8,128)S(1)}, f32[16,32,128]{2,1,0:T(8,128)S(1)}, bf16[32,128,1536]{2,1,0:T(8,128)(2,1)S(1)}, s32[128]{0:T(128)S(4)}, s32[128]{0:T(128)S(4)}) custom-call(s32[128]{0:T(128)} %order_hbm.1, s32[128]{0:T(128)} %counts_hbm.1, f32[1536]{0:T(1024)} %cells_hbm.1, bf16[32,128,1536]{2,1,0:T(8,128)(2,1)} %bitcast.4), custom_call_target="tpu_custom_call" | custom-call | tf_op jit(solution)/shard_map/gram/pallas_call | solution.py:290
  7.3 0.1 collective-permute-start
  7.4 1.5 %collective-permute-done = f32[16,32,128]{2,1,0:T(8,128)S(1)} collective-permute-done((f32[16,32,128]{2,1,0:T(8,128)S(1)}, f32[16,32,128]{2,1,0:T(8,128)S(1)}, u32[]{:S(2)}, u32[]{:S(2)}) %collective-permute-start) | collective-permute-done | bytes 262176 | tf_op jit(solution)/shard_map/ppermute | solution.py:314
  9.0 16.9 %all_to_all.10.parts_ref = f32[16,32,128]{2,1,0:T(8,128)S(1)} all-to-all(f32[16,32,128]{2,1,0:T(8,128)S(1)} %add.34), channel_id=1, replica_groups=mesh['space_0'=4,'space_1'=4,'space_2'=2,'freq'=4] {'space_0','space_1'}, dimensions={0} | all-to-all | bytes 524288 | tf_op jit(solution)/shard_map/all_to_all | solution.py:315
  25.9 4.9 %solve.1 = (bf16[16,80,128]{2,1,0:T(8,128)(2,1)S(1)}, f32[1,64]{1,0:T(1,128)S(1)}) custom-call(s32[128]{0:T(128)S(4)} %get-tuple-element.10.order, s32[128]{0:T(128)S(4)} %get-tuple-element.11.counts, f32[16,32,128]{2,1,0:T(8,128)S(1)} %all_to_all.10.parts_ref), custom_call_target="tpu_custom_call" | custom-call | tf_op jit(solution)/shard_map/solve/pallas_call | solution.py:316
  30.8 11.9 %all_to_all.11.own_ref = bf16[16,80,128]{2,1,0:T(8,128)(2,1)S(1)} all-to-all(bf16[16,80,128]{2,1,0:T(8,128)(2,1)S(1)} %get-tuple-element.14), channel_id=1, replica_groups=mesh['space_0'=4,'space_1'=4,'space_2'=2,'freq'=4] {'space_0','space_1'}, dimensions={0} | all-to-all | bytes 655360 | tf_op jit(solution)/shard_map/all_to_all | solution.py:324
  42.7 0.0 collective-permute-start.1
  42.8 1.6 %collective-permute-done.1.other_ref = bf16[16,80,128]{2,1,0:T(8,128)(2,1)S(1)} collective-permute-done((bf16[16,80,128]{2,1,0:T(8,128)(2,1)S(1)}, bf16[16,80,128]{2,1,0:T(8,128)(2,1)S(1)}, u32[]{:S(2)}, u32[]{:S(2)}) %collective-permute-start.1) | collective-permute-done | bytes 327712 | tf_op jit(solution)/shard_map/ppermute | solution.py:325
  44.4 0.1 add_bitcast_fusion
  44.5 2.8 %collective-permute-start.4 = (f32[64]{0:T(128)S(1)}, f32[64]{0:T(128)S(1)}, u32[]{:S(2)}, u32[]{:S(2)}) collective-permute-start(f32[64]{0:T(128)S(1)} %add_bitcast_fusion), channel_id=1, source_target_pairs={{0,3},{1,0},{2,1},{3,2},{4,7},{5,4},{6,5},{7,6},{8,11},{9,8},{10,9... | collective-permute-start | bytes 776 | tf_op jit(solution)/shard_map/ppermute | solution.py:346
  47.2 0.8 %collective-permute-start.3 = (f32[64]{0:T(128)S(1)}, f32[64]{0:T(128)S(1)}, u32[]{:S(2)}, u32[]{:S(2)}) collective-permute-start(f32[64]{0:T(128)S(1)} %add_bitcast_fusion), channel_id=1, source_target_pairs={{0,2},{1,3},{2,0},{3,1},{4,6},{5,7},{6,4},{7,5},{8,10},{9,11},{10,... | collective-permute-start | bytes 776 | tf_op jit(solution)/shard_map/ppermute | solution.py:346
  48.0 0.9 %collective-permute-start.2 = (f32[64]{0:T(128)S(1)}, f32[64]{0:T(128)S(1)}, u32[]{:S(2)}, u32[]{:S(2)}) collective-permute-start(f32[64]{0:T(128)S(1)} %add_bitcast_fusion), channel_id=1, source_target_pairs={{0,1},{1,2},{2,3},{3,0},{4,5},{5,6},{6,7},{7,4},{8,9},{9,10},{10,1... | collective-permute-start | bytes 776 | tf_op jit(solution)/shard_map/ppermute | solution.py:346
  48.9 0.5 copy.7
  49.5 5.8 %modes.1 = bf16[32,128,1536]{2,1,0:T(8,128)(2,1)} custom-call(s32[128]{0:T(128)S(4)} %get-tuple-element.10.order, bf16[16,80,128]{2,1,0:T(8,128)(2,1)S(1)} %all_to_all.11.own_ref, bf16[16,80,128]{2,1,0:T(8,128)(2,1)S(1)} %collective-permute-done.1.other_ref, bf16[32,128,1536]{2,1,0:T(8,128)(2,1)S(1)} %get-tuple-element.15.kept_ref), custom_call_target="tpu_custom_call" | custom-call | tf_op jit(solution)/shard_map/modes/pallas_call | solution.py:331
  55.3 0.0 collective-permute-done.4
  55.3 0.0 collective-permute-done.3
  55.3 0.0 collective-permute-done.2
  55.3 0.5 add_multiply_fusion
  (3 shorter events, 0.1 us)
Async XLA Ops:
  7.3 1.6 %collective-permute-start = (f32[16,32,128]{2,1,0:T(8,128)S(1)}, f32[16,32,128]{2,1,0:T(8,128)S(1)}, u32[]{:S(2)}, u32[]{:S(2)}) collective-permute-start(f32[16,32,128]{2,1,0:T(8,128)S(1)} %get-tuple-element.13), channel_id=1, source_target_pairs={{0,4},{4,0},{1,5},{5,1},{2,6},{6,2},{3,7},{7,3},{8,12},{12,8},{9,1... | collective-permute-start | bytes 786440 | tf_op jit(solution)/shard_map/ppermute | solution.py:314
  42.7 1.6 %collective-permute-start.1 = (bf16[16,80,128]{2,1,0:T(8,128)(2,1)S(1)}, bf16[16,80,128]{2,1,0:T(8,128)(2,1)S(1)}, u32[]{:S(2)}, u32[]{:S(2)}) collective-permute-start(bf16[16,80,128]{2,1,0:T(8,128)(2,1)S(1)} %all_to_all.11.own_ref), channel_id=1, source_target_pairs={{0,4},{4,0},{1,5},{5,1},{2,6},{6,2},{3,7},{7,3},{8,12},{12,8},{9,1... | collective-permute-start | bytes 983048 | tf_op jit(solution)/shard_map/ppermute | solution.py:325
  44.5 10.8 %collective-permute-start.4 = (f32[64]{0:T(128)S(1)}, f32[64]{0:T(128)S(1)}, u32[]{:S(2)}, u32[]{:S(2)}) collective-permute-start(f32[64]{0:T(128)S(1)} %add_bitcast_fusion), channel_id=1, source_target_pairs={{0,3},{1,0},{2,1},{3,2},{4,7},{5,4},{6,5},{7,6},{8,11},{9,8},{10,9... | collective-permute-start | bytes 776 | tf_op jit(solution)/shard_map/ppermute | solution.py:346
  47.2 8.0 %collective-permute-start.3 = (f32[64]{0:T(128)S(1)}, f32[64]{0:T(128)S(1)}, u32[]{:S(2)}, u32[]{:S(2)}) collective-permute-start(f32[64]{0:T(128)S(1)} %add_bitcast_fusion), channel_id=1, source_target_pairs={{0,2},{1,3},{2,0},{3,1},{4,6},{5,7},{6,4},{7,5},{8,10},{9,11},{10,... | collective-permute-start | bytes 776 | tf_op jit(solution)/shard_map/ppermute | solution.py:346
  48.0 7.3 %collective-permute-start.2 = (f32[64]{0:T(128)S(1)}, f32[64]{0:T(128)S(1)}, u32[]{:S(2)}, u32[]{:S(2)}) collective-permute-start(f32[64]{0:T(128)S(1)} %add_bitcast_fusion), channel_id=1, source_target_pairs={{0,1},{1,2},{2,3},{3,0},{4,5},{5,6},{6,7},{7,4},{8,9},{9,10},{10,1... | collective-permute-start | bytes 776 | tf_op jit(solution)/shard_map/ppermute | solution.py:346

commit v3 on v2

--- a/solution.py
+++ b/solution.py
@@ -156,7 +156,7 @@
             out_ref[i] = packs[place_of(i, half, order, count)]
 
 
-def orth_rows(zt):
+def orth_rows(zt, held):
     n = zt.shape[0]
     gram = nt(zt, zt, HIGH)
     rest_g, rest_z = gram, zt
@@ -167,9 +167,9 @@
         head_g, head_z = rest_g[:BLK], rest_z[:BLK]
         more = n - r0 - BLK
         tail_g, tail_z = (rest_g[BLK:], rest_z[BLK:]) if more else (None, None)
-        cols = [
-            jnp.broadcast_to(head_g[:, r0 + j : r0 + j + 1], (BLK, 128)) for j in range(BLK)
-        ]
+        for j in range(BLK):
+            held[j] = jnp.broadcast_to(head_g[:, r0 + j : r0 + j + 1], (BLK, 128))
+        cols = [held[j] for j in range(BLK)]
         tails = [
             jnp.broadcast_to(tail_g[:, r0 + j : r0 + j + 1], (more, 128)) if more else None
             for j in range(BLK)
@@ -198,7 +198,7 @@
     return jnp.concatenate(outs, axis=0)
 
 
-def solve_kernel(order, counts, parts_ref, pay_ref, ritz_ref):
+def solve_kernel(order, counts, parts_ref, pay_ref, ritz_ref, held):
     summed = parts_ref[0]
     for i in range(1, parts_ref.shape[0]):
         summed = summed + parts_ref[i]
@@ -215,7 +215,7 @@
     start = jnp.where(mild, shifted[:64], eye[:64])
     sweeps = jnp.where(mild, ITERS - 1, ITERS)
     basis = lax.fori_loop(
-        0, sweeps, lambda _, rows: orth_rows(nn(rows, shifted, HIGH)), start
+        0, sweeps, lambda _, rows: orth_rows(nn(rows, shifted, HIGH), held), start
     )
     quad = basis * nn(basis, hermit, HIGH)
     ritz = nt(jnp.ones((8, 128), jnp.float32), quad, HIGH)
@@ -240,35 +240,38 @@
         pay_ref[i, 64:] = tail
 
 
-def modes_kernel(order, own_ref, other_ref, kept_ref, out, expanders, stage, sems):
-    count = kept_ref.shape[0]
+def modes_kernel(half, order, bases_ref, kept_ref, ritz_ref, *rest):
+    if half == 1:
+        out, spectrum, expanders, stage, sems, side = rest
+        show = pltpu.make_async_copy(ritz_ref, spectrum, side)
+        show.start()
+    else:
+        _, out, expanders, stage, sems = rest
+    count = bases_ref.shape[0]
+    group = kept_ref.shape[0]
     _, lane = iotas((64, 128))
-    for half, bases_ref in ((1, own_ref), (0, other_ref)):
-        for i in range(count // 2):
-            k = i + (1 - half) * (count // 2)
-            basis = bases_ref[i, :64].astype(jnp.float32)
-            expanders[k, :64] = jnp.where(lane < 64, basis, -basis).astype(jnp.bfloat16)
-            expanders[k, 64:] = pltpu.roll(basis, 64, 1).astype(jnp.bfloat16)
-    group, core, _ = here()
-
-    def place(k):
-        far = lax.div(k, count // 2)
-        i = k - far * (count // 2)
-        return order[slot_of(i, core + far * (1 - 2 * core), group)] - group * count
+    for i in range(count):
+        basis = bases_ref[i, :64].astype(jnp.float32)
+        expanders[i, :64] = jnp.where(lane < 64, basis, -basis).astype(jnp.bfloat16)
+        expanders[i, 64:] = pltpu.roll(basis, 64, 1).astype(jnp.bfloat16)
 
     def copy(i):
-        return pltpu.make_async_copy(stage.at[i], out.at[place(i)], sems.at[i])
-
-    @pl.loop(0, count, step=UNROLL)
+        dest = out.at[place_of(i, half, order, group)]
+        return pltpu.make_async_copy(stage.at[i], dest, sems.at[i])
+
+    @pl.loop(0, count, step=8)
     def _(i):
-        for j in range(UNROLL):
-            rows = kept_ref[place(i + j)]
+        for j in range(8):
+            rows = kept_ref[place_of(i + j, half, order, group)]
             stage[i + j] = nn(expanders[i + j], rows).astype(jnp.bfloat16)
             copy(i + j).start()
 
     @pl.loop(0, count)
     def _(i):
         copy(i).wait()
+
+    if half == 1:
+        show.wait()
 
 
 def compiler(mib):
@@ -318,6 +321,7 @@
         out_shape=(pltpu.VMEM((plane, PAY, 128), bf16), pltpu.VMEM((1, M), f32)),
         in_specs=[SMEM_SPEC, SMEM_SPEC, VMEM_SPEC],
         out_specs=(VMEM_SPEC, VMEM_SPEC),
+        scratch_shapes=[pltpu.VMEM((BLK, BLK, 128), f32)],
         compiler_params=compiler(16),
         name="solve",
     )(order, counts, parts)
@@ -328,26 +332,39 @@
         tail = b[:, 64:66].astype(f32).sum(axis=0)
         return tail[0, :64] + tail[0, 64:] + tail[1, :64]
 
-    fields = pl.pallas_call(
-        modes_kernel,
-        out_shape=jax.ShapeDtypeStruct((fgroup, 2 * blocks, points), bf16),
-        in_specs=[SMEM_SPEC, VMEM_SPEC, VMEM_SPEC, VMEM_SPEC],
-        out_specs=HBM_SPEC,
-        scratch_shapes=[
-            pltpu.VMEM((fgroup, 128, 128), bf16),
-            pltpu.VMEM((fgroup, 2 * blocks, points), bf16),
-            pltpu.SemaphoreType.DMA((fgroup,)),
-        ],
-        compiler_params=compiler(16),
-        name="modes",
-    )(order, bases, others, kept)
+    def modes(half, bases, *into):
+        out = jax.ShapeDtypeStruct((fgroup, 2 * blocks, points), bf16)
+        shown = jax.ShapeDtypeStruct((1, M), f32)
+        return pl.pallas_call(
+            functools.partial(modes_kernel, half),
+            out_shape=(out, shown) if half == 1 else out,
+            in_specs=[SMEM_SPEC, VMEM_SPEC, VMEM_SPEC, VMEM_SPEC] + [HBM_SPEC] * len(into),
+            out_specs=(HBM_SPEC, HBM_SPEC) if half == 1 else HBM_SPEC,
+            scratch_shapes=[
+                pltpu.VMEM((plane, 128, 128), bf16),
+                pltpu.VMEM((plane, 2 * blocks, points), bf16),
+                pltpu.SemaphoreType.DMA((plane,)),
+            ]
+            + [pltpu.SemaphoreType.DMA] * half,
+            input_output_aliases={4: 0} if into else {},
+            cost_estimate=pl.CostEstimate(
+                flops=2 * plane * 128 * 128 * points,
+                bytes_accessed=plane * 128 * points * 2,
+                transcendentals=0,
+            ),
+            compiler_params=compiler(16),
+            name="modes%d" % half,
+        )(order, bases, kept, ritz, *into)
+
+    fields, spectrum = modes(1, bases)
+    fields = modes(0, others, fields)
     energy = total(bases) + total(others)
     ring = [
         lax.ppermute(energy, "freq", [(i, (i + k) % freqs) for i in range(freqs)])
         for k in range(1, freqs)
     ]
     energy = functools.reduce(jnp.add, ring, energy) / (fgroup * freqs)
-    return (fields.reshape(fgroup, 2, M, points), ritz, energy)
+    return (fields.reshape(fgroup, 2, M, points), spectrum, energy)
 
 
 def solution(mesh):

time: 56.2 us -> 54.8 us (0.975)
  waiting for transfers between devices: 3.13 us -> 2.22 us
    ppermute x1, waiting for transfers between devices: 1.6 us -> 0.01 us  [shards(): others = lax.ppermute(bases, CORE, swap)]
    ppermute x3, waiting for transfers between devices: 0.01 us -> 0.69 us  [shards(): lax.ppermute(energy, 'freq', [(i, (i + k) % freqs) for i in range(freqs)])]
    pallas_call x1 -> x2, Pallas kernels: 5.82 us -> 6.37 us  [modes(): pl.pallas_call(functools.partial(modes_kernel, half), out_shape=(out, sho...]
  transfers between devices with their start and end apart: 5 -> 5, of which waited for: 2 -> 3; matrix products, arithmetic and copies ran while one was open for 1% -> 0% of each run, Pallas kernels for 10% -> 12%
where the time goes in v3:
time: 54.8 us; the launch traced here: 54.6 us
  blocking collectives  28.9 us (53%)
  Pallas kernels  17.6 us (32%)
  starting transfers between devices  4.54 us (8%)
  waiting for transfers between devices  2.22 us (4%)
  other arithmetic  0.69 us (1%)
  between operations  0.68 us (1%)
    all_to_all x1, blocking collectives, shards(): parts = lax.all_to_all(mine, PLANE, 0, 0, tiled=True)  16.9 us
    all_to_all x1, blocking collectives, shards(): bases = lax.all_to_all(payload, PLANE, 0, 0, tiled=True)  11.9 us
    pallas_call x1, Pallas kernels, shards(): pl.pallas_call(gram_kernel, out_shape=(packed, packed, pltpu.VMEM((fgroup...  6.67 us
    pallas_call x2, Pallas kernels, modes(): pl.pallas_call(functools.partial(modes_kernel, half), out_shape=(out, sho...  6.37 us
    pallas_call x1, Pallas kernels, shards(): pl.pallas_call(solve_kernel, out_shape=(pltpu.VMEM((plane, PAY, 128), bf1...  4.53 us
    ppermute x3, starting transfers between devices, shards(): lax.ppermute(energy, 'freq', [(i, (i + k) % freqs) for i in range(freqs)])  4.45 us
    ppermute x1, waiting for transfers between devices, shards(): mine = own + lax.ppermute(send, CORE, swap)  1.52 us
  transfers between devices with their start and end apart: 5, of which 3 were waited for; matrix products, arithmetic and copies ran while one was open for 0% of the time, Pallas kernels for 12%

profile of v3, /device:TPU:0, one launch (start us, length us, event | category | flops | bytes accessed | tf_op | source)
XLA Modules:
  0.0 54.6 jit_solution(16463807478630125239)
XLA Ops:
  0.6 6.7 %gram.1 = (f32[16,32,128]{2,1,0:T(8,128)S(1)}, f32[16,32,128]{2,1,0:T(8,128)S(1)}, bf16[32,128,1536]{2,1,0:T(8,128)(2,1)S(1)}, s32[128]{0:T(128)S(4)}, s32[128]{0:T(128)S(4)}) custom-call(s32[128]{0:T(128)} %order_hbm.1, s32[128]{0:T(128)} %counts_hbm.1, f32[1536]{0:T(1024)} %cells_hbm.1, bf16[32,128,1536]{2,1,0:T(8,128)(2,1)} %bitcast.4), custom_call_target="tpu_custom_call" | custom-call | tf_op jit(solution)/shard_map/gram/pallas_call | solution.py:293
  7.3 0.1 collective-permute-start
  7.4 1.5 %collective-permute-done = f32[16,32,128]{2,1,0:T(8,128)S(1)} collective-permute-done((f32[16,32,128]{2,1,0:T(8,128)S(1)}, f32[16,32,128]{2,1,0:T(8,128)S(1)}, u32[]{:S(2)}, u32[]{:S(2)}) %collective-permute-start) | collective-permute-done | bytes 262176 | tf_op jit(solution)/shard_map/ppermute | solution.py:317
  9.0 16.9 %all_to_all.10.parts_ref = f32[16,32,128]{2,1,0:T(8,128)S(1)} all-to-all(f32[16,32,128]{2,1,0:T(8,128)S(1)} %add.34), channel_id=1, replica_groups=mesh['space_0'=4,'space_1'=4,'space_2'=2,'freq'=4] {'space_0','space_1'}, dimensions={0} | all-to-all | bytes 524288 | tf_op jit(solution)/shard_map/all_to_all | solution.py:318
  25.9 4.5 %solve.1 = (bf16[16,80,128]{2,1,0:T(8,128)(2,1)S(1)}, f32[1,64]{1,0:T(1,128)S(1)}) custom-call(s32[128]{0:T(128)S(4)} %get-tuple-element.12.order, s32[128]{0:T(128)S(4)} %get-tuple-element.13.counts, f32[16,32,128]{2,1,0:T(8,128)S(1)} %all_to_all.10.parts_ref), custom_call_target="tpu_custom_call" | custom-call | tf_op jit(solution)/shard_map/solve/pallas_call | solution.py:319
  30.4 11.9 %all_to_all.11.bases_ref = bf16[16,80,128]{2,1,0:T(8,128)(2,1)S(1)} all-to-all(bf16[16,80,128]{2,1,0:T(8,128)(2,1)S(1)} %get-tuple-element.16), channel_id=1, replica_groups=mesh['space_0'=4,'space_1'=4,'space_2'=2,'freq'=4] {'space_0','space_1'}, dimensions={0} | all-to-all | bytes 655360 | tf_op jit(solution)/shard_map/all_to_all | solution.py:328
  42.4 0.0 collective-permute-start.1
  42.4 3.2 %modes1.1 = (bf16[32,128,1536]{2,1,0:T(8,128)(2,1)}, f32[1,64]{1,0:T(1,128)}) custom-call(s32[128]{0:T(128)S(4)} %get-tuple-element.12.order, bf16[16,80,128]{2,1,0:T(8,128)(2,1)S(1)} %all_to_all.11.bases_ref, bf16[32,128,1536]{2,1,0:T(8,128)(2,1)S(1)} %get-tuple-element.17.kept_ref, f32[1,64]{1,0:T(1,128)S(1)} %get-tuple-element.18.ritz_ref), custom_call_target="tpu_custom_call" | custom-call | flops 805306368 | bytes 6291456 | tf_op jit(solution)/shard_map/modes1/pallas_call | solution.py:338
  45.6 0.0 collective-permute-done.1.bases_ref
  45.6 0.1 add_bitcast_fusion
  45.7 2.8 %collective-permute-start.4 = (f32[64]{0:T(128)S(1)}, f32[64]{0:T(128)S(1)}, u32[]{:S(2)}, u32[]{:S(2)}) collective-permute-start(f32[64]{0:T(128)S(1)} %add_bitcast_fusion), channel_id=1, source_target_pairs={{0,3},{1,0},{2,1},{3,2},{4,7},{5,4},{6,5},{7,6},{8,11},{9,8},{10,9... | collective-permute-start | bytes 776 | tf_op jit(solution)/shard_map/ppermute | solution.py:363
  48.5 0.8 %collective-permute-start.3 = (f32[64]{0:T(128)S(1)}, f32[64]{0:T(128)S(1)}, u32[]{:S(2)}, u32[]{:S(2)}) collective-permute-start(f32[64]{0:T(128)S(1)} %add_bitcast_fusion), channel_id=1, source_target_pairs={{0,2},{1,3},{2,0},{3,1},{4,6},{5,7},{6,4},{7,5},{8,10},{9,11},{10,... | collective-permute-start | bytes 776 | tf_op jit(solution)/shard_map/ppermute | solution.py:363
  49.3 0.9 %collective-permute-start.2 = (f32[64]{0:T(128)S(1)}, f32[64]{0:T(128)S(1)}, u32[]{:S(2)}, u32[]{:S(2)}) collective-permute-start(f32[64]{0:T(128)S(1)} %add_bitcast_fusion), channel_id=1, source_target_pairs={{0,1},{1,2},{2,3},{3,0},{4,5},{5,6},{6,7},{7,4},{8,9},{9,10},{10,1... | collective-permute-start | bytes 776 | tf_op jit(solution)/shard_map/ppermute | solution.py:363
  50.2 3.2 %modes0.1 = bf16[32,128,1536]{2,1,0:T(8,128)(2,1)} custom-call(s32[128]{0:T(128)S(4)} %get-tuple-element.12.order, bf16[16,80,128]{2,1,0:T(8,128)(2,1)S(1)} %collective-permute-done.1.bases_ref, bf16[32,128,1536]{2,1,0:T(8,128)(2,1)S(1)} %get-tuple-element.17.kept_ref, f32[1,64]{1,0:T(1,128)S(1)} %get-tuple-element.18.ritz_ref, ...), custom_call_target="tpu_custom_call", output_to_operand_aliasing={{}: (4, {})} | custom-call | flops 805306368 | bytes 6291456 | tf_op jit(solution)/shard_map/modes0/pallas_call | solution.py:338
  53.4 0.0 collective-permute-done.4
  53.4 0.2 collective-permute-done.3
  53.6 0.5 collective-permute-done.2
  54.1 0.5 add_multiply_fusion
  (3 shorter events, 0.1 us)
Async XLA Ops:
  7.3 1.6 %collective-permute-start = (f32[16,32,128]{2,1,0:T(8,128)S(1)}, f32[16,32,128]{2,1,0:T(8,128)S(1)}, u32[]{:S(2)}, u32[]{:S(2)}) collective-permute-start(f32[16,32,128]{2,1,0:T(8,128)S(1)} %get-tuple-element.15), channel_id=1, source_target_pairs={{0,4},{4,0},{1,5},{5,1},{2,6},{6,2},{3,7},{7,3},{8,12},{12,8},{9,1... | collective-permute-start | bytes 786440 | tf_op jit(solution)/shard_map/ppermute | solution.py:317
  42.4 3.2 %collective-permute-start.1 = (bf16[16,80,128]{2,1,0:T(8,128)(2,1)S(1)}, bf16[16,80,128]{2,1,0:T(8,128)(2,1)S(1)}, u32[]{:S(2)}, u32[]{:S(2)}) collective-permute-start(bf16[16,80,128]{2,1,0:T(8,128)(2,1)S(1)} %all_to_all.11.bases_ref), channel_id=1, source_target_pairs={{0,4},{4,0},{1,5},{5,1},{2,6},{6,2},{3,7},{7,3},{8,12},{12,8},{9,1... | collective-permute-start | bytes 983048 | tf_op jit(solution)/shard_map/ppermute | solution.py:329
  45.7 7.6 %collective-permute-start.4 = (f32[64]{0:T(128)S(1)}, f32[64]{0:T(128)S(1)}, u32[]{:S(2)}, u32[]{:S(2)}) collective-permute-start(f32[64]{0:T(128)S(1)} %add_bitcast_fusion), channel_id=1, source_target_pairs={{0,3},{1,0},{2,1},{3,2},{4,7},{5,4},{6,5},{7,6},{8,11},{9,8},{10,9... | collective-permute-start | bytes 776 | tf_op jit(solution)/shard_map/ppermute | solution.py:363
  48.5 5.1 %collective-permute-start.3 = (f32[64]{0:T(128)S(1)}, f32[64]{0:T(128)S(1)}, u32[]{:S(2)}, u32[]{:S(2)}) collective-permute-start(f32[64]{0:T(128)S(1)} %add_bitcast_fusion), channel_id=1, source_target_pairs={{0,2},{1,3},{2,0},{3,1},{4,6},{5,7},{6,4},{7,5},{8,10},{9,11},{10,... | collective-permute-start | bytes 776 | tf_op jit(solution)/shard_map/ppermute | solution.py:363
  49.3 4.8 %collective-permute-start.2 = (f32[64]{0:T(128)S(1)}, f32[64]{0:T(128)S(1)}, u32[]{:S(2)}, u32[]{:S(2)}) collective-permute-start(f32[64]{0:T(128)S(1)} %add_bitcast_fusion), channel_id=1, source_target_pairs={{0,1},{1,2},{2,3},{3,0},{4,5},{5,6},{6,7},{7,4},{8,9},{9,10},{10,1... | collective-permute-start | bytes 776 | tf_op jit(solution)/shard_map/ppermute | solution.py:363

commit v4 on v3

--- a/solution.py
+++ b/solution.py
@@ -16,7 +16,7 @@
 SPACE_FREQ = ("space_0", "space_1", "space_2", "freq")
 HIGH = lax.Precision.HIGHEST
 BLK = 16
-PAY = 80
+PAY = 72
 UNROLL = 4
 FLIGHT = 4
 
@@ -234,7 +234,7 @@
     upper = jnp.concatenate([one.astype(jnp.float32), two.astype(jnp.float32)], axis=1)
     lower = jnp.concatenate([three, jnp.zeros_like(three)], axis=1)
     tail = jnp.where(row == 0, upper, jnp.where(row == 1, lower, 0.0))
-    tail = jnp.concatenate([tail, jnp.zeros((8, 128), jnp.float32)], axis=0).astype(jnp.bfloat16)
+    tail = tail.astype(jnp.bfloat16)
     for i in range(pay_ref.shape[0]):
         pay_ref[i, :64] = sent
         pay_ref[i, 64:] = tail

time: 54.8 us -> 54.6 us (level)
  no operation moved by 1% of the time
where the time goes in v4:
time: 54.6 us; the launch traced here: 54.4 us
  blocking collectives  28.7 us (53%)
  Pallas kernels  17.6 us (32%)
  starting transfers between devices  4.54 us (8%)
  waiting for transfers between devices  2.22 us (4%)
  other arithmetic  0.69 us (1%)
  between operations  0.68 us (1%)
    all_to_all x1, blocking collectives, shards(): parts = lax.all_to_all(mine, PLANE, 0, 0, tiled=True)  16.9 us
    all_to_all x1, blocking collectives, shards(): bases = lax.all_to_all(payload, PLANE, 0, 0, tiled=True)  11.8 us
    pallas_call x1, Pallas kernels, shards(): pl.pallas_call(gram_kernel, out_shape=(packed, packed, pltpu.VMEM((fgroup...  6.67 us
    pallas_call x2, Pallas kernels, modes(): pl.pallas_call(functools.partial(modes_kernel, half), out_shape=(out, sho...  6.37 us
    pallas_call x1, Pallas kernels, shards(): pl.pallas_call(solve_kernel, out_shape=(pltpu.VMEM((plane, PAY, 128), bf1...  4.53 us
    ppermute x3, starting transfers between devices, shards(): lax.ppermute(energy, 'freq', [(i, (i + k) % freqs) for i in range(freqs)])  4.45 us
    ppermute x1, waiting for transfers between devices, shards(): mine = own + lax.ppermute(send, CORE, swap)  1.52 us
  transfers between devices with their start and end apart: 5, of which 3 were waited for; matrix products, arithmetic and copies ran while one was open for 0% of the time, Pallas kernels for 12%

profile of v4, /device:TPU:0, one launch (start us, length us, event | category | flops | bytes accessed | tf_op | source)
XLA Modules:
  0.0 54.4 jit_solution(194755201484647447)
XLA Ops:
  0.6 6.7 %gram.1 = (f32[16,32,128]{2,1,0:T(8,128)S(1)}, f32[16,32,128]{2,1,0:T(8,128)S(1)}, bf16[32,128,1536]{2,1,0:T(8,128)(2,1)S(1)}, s32[128]{0:T(128)S(4)}, s32[128]{0:T(128)S(4)}) custom-call(s32[128]{0:T(128)} %order_hbm.1, s32[128]{0:T(128)} %counts_hbm.1, f32[1536]{0:T(1024)} %cells_hbm.1, bf16[32,128,1536]{2,1,0:T(8,128)(2,1)} %bitcast.4), custom_call_target="tpu_custom_call" | custom-call | tf_op jit(solution)/shard_map/gram/pallas_call | solution.py:293
  7.3 0.1 collective-permute-start
  7.4 1.5 %collective-permute-done = f32[16,32,128]{2,1,0:T(8,128)S(1)} collective-permute-done((f32[16,32,128]{2,1,0:T(8,128)S(1)}, f32[16,32,128]{2,1,0:T(8,128)S(1)}, u32[]{:S(2)}, u32[]{:S(2)}) %collective-permute-start) | collective-permute-done | bytes 262176 | tf_op jit(solution)/shard_map/ppermute | solution.py:317
  9.0 16.9 %all_to_all.10.parts_ref = f32[16,32,128]{2,1,0:T(8,128)S(1)} all-to-all(f32[16,32,128]{2,1,0:T(8,128)S(1)} %add.34), channel_id=1, replica_groups=mesh['space_0'=4,'space_1'=4,'space_2'=2,'freq'=4] {'space_0','space_1'}, dimensions={0} | all-to-all | bytes 524288 | tf_op jit(solution)/shard_map/all_to_all | solution.py:318
  25.9 4.5 %solve.1 = (bf16[16,72,128]{2,1,0:T(8,128)(2,1)S(1)}, f32[1,64]{1,0:T(1,128)S(1)}) custom-call(s32[128]{0:T(128)S(4)} %get-tuple-element.12.order, s32[128]{0:T(128)S(4)} %get-tuple-element.13.counts, f32[16,32,128]{2,1,0:T(8,128)S(1)} %all_to_all.10.parts_ref), custom_call_target="tpu_custom_call" | custom-call | tf_op jit(solution)/shard_map/solve/pallas_call | solution.py:319
  30.4 11.8 %all_to_all.11.bases_ref = bf16[16,72,128]{2,1,0:T(8,128)(2,1)S(1)} all-to-all(bf16[16,72,128]{2,1,0:T(8,128)(2,1)S(1)} %get-tuple-element.16), channel_id=1, replica_groups=mesh['space_0'=4,'space_1'=4,'space_2'=2,'freq'=4] {'space_0','space_1'}, dimensions={0} | all-to-all | bytes 589824 | tf_op jit(solution)/shard_map/all_to_all | solution.py:328
  42.2 0.0 collective-permute-start.1
  42.2 3.2 %modes1.1 = (bf16[32,128,1536]{2,1,0:T(8,128)(2,1)}, f32[1,64]{1,0:T(1,128)}) custom-call(s32[128]{0:T(128)S(4)} %get-tuple-element.12.order, bf16[16,72,128]{2,1,0:T(8,128)(2,1)S(1)} %all_to_all.11.bases_ref, bf16[32,128,1536]{2,1,0:T(8,128)(2,1)S(1)} %get-tuple-element.17.kept_ref, f32[1,64]{1,0:T(1,128)S(1)} %get-tuple-element.18.ritz_ref), custom_call_target="tpu_custom_call" | custom-call | flops 805306368 | bytes 6291456 | tf_op jit(solution)/shard_map/modes1/pallas_call | solution.py:338
  45.4 0.0 collective-permute-done.1.bases_ref
  45.5 0.1 add_bitcast_fusion
  45.5 2.8 %collective-permute-start.4 = (f32[64]{0:T(128)S(1)}, f32[64]{0:T(128)S(1)}, u32[]{:S(2)}, u32[]{:S(2)}) collective-permute-start(f32[64]{0:T(128)S(1)} %add_bitcast_fusion), channel_id=1, source_target_pairs={{0,3},{1,0},{2,1},{3,2},{4,7},{5,4},{6,5},{7,6},{8,11},{9,8},{10,9... | collective-permute-start | bytes 776 | tf_op jit(solution)/shard_map/ppermute | solution.py:363
  48.3 0.8 %collective-permute-start.3 = (f32[64]{0:T(128)S(1)}, f32[64]{0:T(128)S(1)}, u32[]{:S(2)}, u32[]{:S(2)}) collective-permute-start(f32[64]{0:T(128)S(1)} %add_bitcast_fusion), channel_id=1, source_target_pairs={{0,2},{1,3},{2,0},{3,1},{4,6},{5,7},{6,4},{7,5},{8,10},{9,11},{10,... | collective-permute-start | bytes 776 | tf_op jit(solution)/shard_map/ppermute | solution.py:363
  49.1 0.9 %collective-permute-start.2 = (f32[64]{0:T(128)S(1)}, f32[64]{0:T(128)S(1)}, u32[]{:S(2)}, u32[]{:S(2)}) collective-permute-start(f32[64]{0:T(128)S(1)} %add_bitcast_fusion), channel_id=1, source_target_pairs={{0,1},{1,2},{2,3},{3,0},{4,5},{5,6},{6,7},{7,4},{8,9},{9,10},{10,1... | collective-permute-start | bytes 776 | tf_op jit(solution)/shard_map/ppermute | solution.py:363
  50.0 3.2 %modes0.1 = bf16[32,128,1536]{2,1,0:T(8,128)(2,1)} custom-call(s32[128]{0:T(128)S(4)} %get-tuple-element.12.order, bf16[16,72,128]{2,1,0:T(8,128)(2,1)S(1)} %collective-permute-done.1.bases_ref, bf16[32,128,1536]{2,1,0:T(8,128)(2,1)S(1)} %get-tuple-element.17.kept_ref, f32[1,64]{1,0:T(1,128)S(1)} %get-tuple-element.18.ritz_ref, ...), custom_call_target="tpu_custom_call", output_to_operand_aliasing={{}: (4, {})} | custom-call | flops 805306368 | bytes 6291456 | tf_op jit(solution)/shard_map/modes0/pallas_call | solution.py:338
  53.2 0.0 collective-permute-done.4
  53.2 0.2 collective-permute-done.3
  53.4 0.5 collective-permute-done.2
  53.9 0.5 add_multiply_fusion
  (3 shorter events, 0.1 us)
Async XLA Ops:
  7.3 1.6 %collective-permute-start = (f32[16,32,128]{2,1,0:T(8,128)S(1)}, f32[16,32,128]{2,1,0:T(8,128)S(1)}, u32[]{:S(2)}, u32[]{:S(2)}) collective-permute-start(f32[16,32,128]{2,1,0:T(8,128)S(1)} %get-tuple-element.15), channel_id=1, source_target_pairs={{0,4},{4,0},{1,5},{5,1},{2,6},{6,2},{3,7},{7,3},{8,12},{12,8},{9,1... | collective-permute-start | bytes 786440 | tf_op jit(solution)/shard_map/ppermute | solution.py:317
  42.2 3.2 %collective-permute-start.1 = (bf16[16,72,128]{2,1,0:T(8,128)(2,1)S(1)}, bf16[16,72,128]{2,1,0:T(8,128)(2,1)S(1)}, u32[]{:S(2)}, u32[]{:S(2)}) collective-permute-start(bf16[16,72,128]{2,1,0:T(8,128)(2,1)S(1)} %all_to_all.11.bases_ref), channel_id=1, source_target_pairs={{0,4},{4,0},{1,5},{5,1},{2,6},{6,2},{3,7},{7,3},{8,12},{12,8},{9,1... | collective-permute-start | bytes 884744 | tf_op jit(solution)/shard_map/ppermute | solution.py:329
  45.5 7.6 %collective-permute-start.4 = (f32[64]{0:T(128)S(1)}, f32[64]{0:T(128)S(1)}, u32[]{:S(2)}, u32[]{:S(2)}) collective-permute-start(f32[64]{0:T(128)S(1)} %add_bitcast_fusion), channel_id=1, source_target_pairs={{0,3},{1,0},{2,1},{3,2},{4,7},{5,4},{6,5},{7,6},{8,11},{9,8},{10,9... | collective-permute-start | bytes 776 | tf_op jit(solution)/shard_map/ppermute | solution.py:363
  48.3 5.1 %collective-permute-start.3 = (f32[64]{0:T(128)S(1)}, f32[64]{0:T(128)S(1)}, u32[]{:S(2)}, u32[]{:S(2)}) collective-permute-start(f32[64]{0:T(128)S(1)} %add_bitcast_fusion), channel_id=1, source_target_pairs={{0,2},{1,3},{2,0},{3,1},{4,6},{5,7},{6,4},{7,5},{8,10},{9,11},{10,... | collective-permute-start | bytes 776 | tf_op jit(solution)/shard_map/ppermute | solution.py:363
  49.1 4.8 %collective-permute-start.2 = (f32[64]{0:T(128)S(1)}, f32[64]{0:T(128)S(1)}, u32[]{:S(2)}, u32[]{:S(2)}) collective-permute-start(f32[64]{0:T(128)S(1)} %add_bitcast_fusion), channel_id=1, source_target_pairs={{0,1},{1,2},{2,3},{3,0},{4,5},{5,6},{6,7},{7,4},{8,9},{9,10},{10,1... | collective-permute-start | bytes 776 | tf_op jit(solution)/shard_map/ppermute | solution.py:363

commit v5 on v4

--- a/solution.py
+++ b/solution.py
@@ -359,11 +359,10 @@
     fields, spectrum = modes(1, bases)
     fields = modes(0, others, fields)
     energy = total(bases) + total(others)
-    ring = [
-        lax.ppermute(energy, "freq", [(i, (i + k) % freqs) for i in range(freqs)])
-        for k in range(1, freqs)
-    ]
-    energy = functools.reduce(jnp.add, ring, energy) / (fgroup * freqs)
+    one, two, three = (
+        lax.ppermute(energy, "freq", [(i, i ^ k) for i in range(freqs)]) for k in (1, 2, 3)
+    )
+    energy = ((energy + one) + (two + three)) / (fgroup * freqs)
     return (fields.reshape(fgroup, 2, M, points), spectrum, energy)
 
 

time: 54.6 us -> 54.1 us (level)
  transfers between devices with their start and end apart: 5 -> 5, of which waited for: 3 -> 2; matrix products, arithmetic and copies ran while one was open for 0% -> 0% of each run, Pallas kernels for 12% -> 12%
where the time goes in v5:
time: 54.1 us; the launch traced here: 53.9 us
  blocking collectives  28.7 us (53%)
  Pallas kernels  17.6 us (33%)
  starting transfers between devices  4.2 us (8%)
  waiting for transfers between devices  2.07 us (4%)
  other arithmetic  0.69 us (1%)
  between operations  0.68 us (1%)
    all_to_all x1, blocking collectives, shards(): parts = lax.all_to_all(mine, PLANE, 0, 0, tiled=True)  16.9 us
    all_to_all x1, blocking collectives, shards(): bases = lax.all_to_all(payload, PLANE, 0, 0, tiled=True)  11.8 us
    pallas_call x1, Pallas kernels, shards(): pl.pallas_call(gram_kernel, out_shape=(packed, packed, pltpu.VMEM((fgroup...  6.67 us
    pallas_call x2, Pallas kernels, modes(): pl.pallas_call(functools.partial(modes_kernel, half), out_shape=(out, sho...  6.37 us
    pallas_call x1, Pallas kernels, shards(): pl.pallas_call(solve_kernel, out_shape=(pltpu.VMEM((plane, PAY, 128), bf1...  4.53 us
    ppermute x3, starting transfers between devices, shards(): lax.ppermute(energy, 'freq', [(i, i ^ k) for i in range(freqs)])  4.11 us
    ppermute x1, waiting for transfers between devices, shards(): mine = own + lax.ppermute(send, CORE, swap)  1.52 us
  transfers between devices with their start and end apart: 5, of which 2 were waited for; matrix products, arithmetic and copies ran while one was open for 0% of the time, Pallas kernels for 12%

profile of v5, /device:TPU:0, one launch (start us, length us, event | category | flops | bytes accessed | tf_op | source)
XLA Modules:
  0.0 53.9 jit_solution(13101522127299491146)
XLA Ops:
  0.6 6.7 %gram.1 = (f32[16,32,128]{2,1,0:T(8,128)S(1)}, f32[16,32,128]{2,1,0:T(8,128)S(1)}, bf16[32,128,1536]{2,1,0:T(8,128)(2,1)S(1)}, s32[128]{0:T(128)S(4)}, s32[128]{0:T(128)S(4)}) custom-call(s32[128]{0:T(128)} %order_hbm.1, s32[128]{0:T(128)} %counts_hbm.1, f32[1536]{0:T(1024)} %cells_hbm.1, bf16[32,128,1536]{2,1,0:T(8,128)(2,1)} %bitcast.4), custom_call_target="tpu_custom_call" | custom-call | tf_op jit(solution)/shard_map/gram/pallas_call | solution.py:293
  7.3 0.1 collective-permute-start
  7.4 1.5 %collective-permute-done = f32[16,32,128]{2,1,0:T(8,128)S(1)} collective-permute-done((f32[16,32,128]{2,1,0:T(8,128)S(1)}, f32[16,32,128]{2,1,0:T(8,128)S(1)}, u32[]{:S(2)}, u32[]{:S(2)}) %collective-permute-start) | collective-permute-done | bytes 262176 | tf_op jit(solution)/shard_map/ppermute | solution.py:317
  9.0 16.9 %all_to_all.10.parts_ref = f32[16,32,128]{2,1,0:T(8,128)S(1)} all-to-all(f32[16,32,128]{2,1,0:T(8,128)S(1)} %add.34), channel_id=1, replica_groups=mesh['space_0'=4,'space_1'=4,'space_2'=2,'freq'=4] {'space_0','space_1'}, dimensions={0} | all-to-all | bytes 524288 | tf_op jit(solution)/shard_map/all_to_all | solution.py:318
  25.9 4.5 %solve.1 = (bf16[16,72,128]{2,1,0:T(8,128)(2,1)S(1)}, f32[1,64]{1,0:T(1,128)S(1)}) custom-call(s32[128]{0:T(128)S(4)} %get-tuple-element.12.order, s32[128]{0:T(128)S(4)} %get-tuple-element.13.counts, f32[16,32,128]{2,1,0:T(8,128)S(1)} %all_to_all.10.parts_ref), custom_call_target="tpu_custom_call" | custom-call | tf_op jit(solution)/shard_map/solve/pallas_call | solution.py:319
  30.4 11.8 %all_to_all.11.bases_ref = bf16[16,72,128]{2,1,0:T(8,128)(2,1)S(1)} all-to-all(bf16[16,72,128]{2,1,0:T(8,128)(2,1)S(1)} %get-tuple-element.16), channel_id=1, replica_groups=mesh['space_0'=4,'space_1'=4,'space_2'=2,'freq'=4] {'space_0','space_1'}, dimensions={0} | all-to-all | bytes 589824 | tf_op jit(solution)/shard_map/all_to_all | solution.py:328
  42.2 0.0 collective-permute-start.1
  42.2 3.2 %modes1.1 = (bf16[32,128,1536]{2,1,0:T(8,128)(2,1)}, f32[1,64]{1,0:T(1,128)}) custom-call(s32[128]{0:T(128)S(4)} %get-tuple-element.12.order, bf16[16,72,128]{2,1,0:T(8,128)(2,1)S(1)} %all_to_all.11.bases_ref, bf16[32,128,1536]{2,1,0:T(8,128)(2,1)S(1)} %get-tuple-element.17.kept_ref, f32[1,64]{1,0:T(1,128)S(1)} %get-tuple-element.18.ritz_ref), custom_call_target="tpu_custom_call" | custom-call | flops 805306368 | bytes 6291456 | tf_op jit(solution)/shard_map/modes1/pallas_call | solution.py:338
  45.4 0.0 collective-permute-done.1.bases_ref
  45.5 0.1 add_bitcast_fusion
  45.5 2.8 %collective-permute-start.4 = (f32[64]{0:T(128)S(1)}, f32[64]{0:T(128)S(1)}, u32[]{:S(2)}, u32[]{:S(2)}) collective-permute-start(f32[64]{0:T(128)S(1)} %add_bitcast_fusion), channel_id=1, source_target_pairs={{0,3},{1,2},{2,1},{3,0},{4,7},{5,6},{6,5},{7,4},{8,11},{9,10},{10,... | collective-permute-start | bytes 776 | tf_op jit(solution)/shard_map/ppermute | solution.py:363
  48.3 0.8 %collective-permute-start.3 = (f32[64]{0:T(128)S(1)}, f32[64]{0:T(128)S(1)}, u32[]{:S(2)}, u32[]{:S(2)}) collective-permute-start(f32[64]{0:T(128)S(1)} %add_bitcast_fusion), channel_id=1, source_target_pairs={{0,2},{1,3},{2,0},{3,1},{4,6},{5,7},{6,4},{7,5},{8,10},{9,11},{10,... | collective-permute-start | bytes 776 | tf_op jit(solution)/shard_map/ppermute | solution.py:363
  49.1 0.5 %collective-permute-start.2 = (f32[64]{0:T(128)S(1)}, f32[64]{0:T(128)S(1)}, u32[]{:S(2)}, u32[]{:S(2)}) collective-permute-start(f32[64]{0:T(128)S(1)} %add_bitcast_fusion), channel_id=1, source_target_pairs={{0,1},{1,0},{2,3},{3,2},{4,5},{5,4},{6,7},{7,6},{8,9},{9,8},{10,11... | collective-permute-start | bytes 776 | tf_op jit(solution)/shard_map/ppermute | solution.py:363
  49.7 3.2 %modes0.1 = bf16[32,128,1536]{2,1,0:T(8,128)(2,1)} custom-call(s32[128]{0:T(128)S(4)} %get-tuple-element.12.order, bf16[16,72,128]{2,1,0:T(8,128)(2,1)S(1)} %collective-permute-done.1.bases_ref, bf16[32,128,1536]{2,1,0:T(8,128)(2,1)S(1)} %get-tuple-element.17.kept_ref, f32[1,64]{1,0:T(1,128)S(1)} %get-tuple-element.18.ritz_ref, ...), custom_call_target="tpu_custom_call", output_to_operand_aliasing={{}: (4, {})} | custom-call | flops 805306368 | bytes 6291456 | tf_op jit(solution)/shard_map/modes0/pallas_call | solution.py:338
  52.8 0.0 collective-permute-done.4
  52.8 0.5 %collective-permute-done.3 = f32[64]{0:T(128)S(1)} collective-permute-done((f32[64]{0:T(128)S(1)}, f32[64]{0:T(128)S(1)}, u32[]{:S(2)}, u32[]{:S(2)}) %collective-permute-start.3) | collective-permute-done | bytes 288 | tf_op jit(solution)/shard_map/ppermute | solution.py:363
  53.4 0.0 collective-permute-done.2
  53.4 0.5 add_multiply_fusion
  (3 shorter events, 0.1 us)
Async XLA Ops:
  7.3 1.6 %collective-permute-start = (f32[16,32,128]{2,1,0:T(8,128)S(1)}, f32[16,32,128]{2,1,0:T(8,128)S(1)}, u32[]{:S(2)}, u32[]{:S(2)}) collective-permute-start(f32[16,32,128]{2,1,0:T(8,128)S(1)} %get-tuple-element.15), channel_id=1, source_target_pairs={{0,4},{4,0},{1,5},{5,1},{2,6},{6,2},{3,7},{7,3},{8,12},{12,8},{9,1... | collective-permute-start | bytes 786440 | tf_op jit(solution)/shard_map/ppermute | solution.py:317
  42.2 3.2 %collective-permute-start.1 = (bf16[16,72,128]{2,1,0:T(8,128)(2,1)S(1)}, bf16[16,72,128]{2,1,0:T(8,128)(2,1)S(1)}, u32[]{:S(2)}, u32[]{:S(2)}) collective-permute-start(bf16[16,72,128]{2,1,0:T(8,128)(2,1)S(1)} %all_to_all.11.bases_ref), channel_id=1, source_target_pairs={{0,4},{4,0},{1,5},{5,1},{2,6},{6,2},{3,7},{7,3},{8,12},{12,8},{9,1... | collective-permute-start | bytes 884744 | tf_op jit(solution)/shard_map/ppermute | solution.py:329
  45.5 7.3 %collective-permute-start.4 = (f32[64]{0:T(128)S(1)}, f32[64]{0:T(128)S(1)}, u32[]{:S(2)}, u32[]{:S(2)}) collective-permute-start(f32[64]{0:T(128)S(1)} %add_bitcast_fusion), channel_id=1, source_target_pairs={{0,3},{1,2},{2,1},{3,0},{4,7},{5,6},{6,5},{7,4},{8,11},{9,10},{10,... | collective-permute-start | bytes 776 | tf_op jit(solution)/shard_map/ppermute | solution.py:363
  48.3 5.1 %collective-permute-start.3 = (f32[64]{0:T(128)S(1)}, f32[64]{0:T(128)S(1)}, u32[]{:S(2)}, u32[]{:S(2)}) collective-permute-start(f32[64]{0:T(128)S(1)} %add_bitcast_fusion), channel_id=1, source_target_pairs={{0,2},{1,3},{2,0},{3,1},{4,6},{5,7},{6,4},{7,5},{8,10},{9,11},{10,... | collective-permute-start | bytes 776 | tf_op jit(solution)/shard_map/ppermute | solution.py:363
  49.1 4.3 %collective-permute-start.2 = (f32[64]{0:T(128)S(1)}, f32[64]{0:T(128)S(1)}, u32[]{:S(2)}, u32[]{:S(2)}) collective-permute-start(f32[64]{0:T(128)S(1)} %add_bitcast_fusion), channel_id=1, source_target_pairs={{0,1},{1,0},{2,3},{3,2},{4,5},{5,4},{6,7},{7,6},{8,9},{9,8},{10,11... | collective-permute-start | bytes 776 | tf_op jit(solution)/shard_map/ppermute | solution.py:363
